TPU v7x, 256 devices: a whole 4x4x8 slice. The times are simulated.
256 devices in a mesh: section: 8 (over y, core), mp: 32 (over x, z).
Axes of the slice: x: 4, y: 4, z: 8, core: 2. Of those that a mesh axis runs over, the one named last changes fastest.
Arguments:
- arriving: bfloat16 [8, 768, 8192], P('section', None, 'mp'), may hold values from -6 to 6
- norm_gain: bfloat16 [8, 8192], P('section'), may hold values from 0.099609375 to 1.8984375
- w_query: bfloat16 [8, 8192, 8192], P('section', 'mp'), may hold values from -26 to 26
- w_key: bfloat16 [8, 1024, 8192], P('section', 'mp'), may hold values from -1 to 1
- w_value: bfloat16 [8, 1024, 8192], P('section', 'mp'), may hold values from -0.25 to 0.25
- w_out: bfloat16 [8, 8192, 8192], P('section', 'mp'), may hold values from -0.0625 to 0.0625
Outputs:
- attended: bfloat16 [8, 768, 8192], P('section', 'mp')
- stream_next: bfloat16 [8, 768, 8192], P('section', 'mp')
All inputs are finite; a program needn't handle non-finite values.
Results may differ from a plain program's by a relative error of at most 0.017.
Values may be sent and summed in bfloat16 or wider, within the bound.
A program may use at most 128 MiB of HBM per device.

v0:
```python
import math

import jax
import jax.numpy as jnp
from jax import lax
from jax.sharding import Mesh
from jax.sharding import PartitionSpec as P

HD = 128
KV_HEADS = 8
MP = ("mp_0", "mp_1")


rope_base = 500000.0
norm_eps = 1e-05


def shifted(block, axis, distance):
    devices = range(lax.axis_size(axis))
    route = [((i - distance) % len(devices), i) for i in devices]
    return lax.ppermute(block, axis, route)


def sent_together(arrays, axis, dim, along):
    both = jnp.concatenate(arrays, axis=along)
    result, at, outs = (lax.all_gather(both, axis, axis=dim, tiled=True), 0, [])
    for a in arrays:
        outs.append(lax.slice_in_dim(result, at, at + a.shape[along], axis=along))
        at += a.shape[along]
    return tuple(outs)


def scatter_axes(array, axes, dim):
    for axis in axes:
        array = lax.psum_scatter(array, axis, scatter_dimension=dim, tiled=True)
    return array


def rotate_pairs(channel_major, pair_ids):
    channels = channel_major.shape[0]
    length = channel_major.shape[1]
    frequency = jnp.exp(pair_ids.astype(jnp.float32) * (-2.0 * math.log(rope_base) / HD))
    positions = jnp.arange(length, dtype=jnp.int32).astype(jnp.float32)
    angles = frequency[:, None] * positions[None, :]
    cos_table = jnp.cos(angles)
    sine_table = jnp.sin(angles)
    paired = channel_major.reshape(channels // 2, 2, length)
    even_part = paired[:, 0]
    odd_part = paired[:, 1]
    rotated = jnp.stack(
        [
            even_part * cos_table - odd_part * sine_table,
            even_part * sine_table + odd_part * cos_table,
        ],
        axis=1,
    )
    return rotated.reshape(channels, length)


def head_rows(table, kv_index):
    length = table.shape[1]
    grouped = table.reshape(HD // 2, KV_HEADS, 2, length)
    picked = lax.dynamic_slice_in_dim(grouped, kv_index, 1, 1)
    return picked.reshape(HD, length)


def normalize(hidden_in, gain_row):
    as_float = hidden_in.astype(jnp.float32)
    mean_square = jnp.mean(as_float * as_float, axis=1, keepdims=True)
    normed = (as_float * lax.rsqrt(mean_square + norm_eps) * gain_row).astype(jnp.bfloat16)
    return (as_float, normed)


def channel_product(weights, normed):
    return lax.dot_general(
        weights, normed, (((1,), (1,)), ((), ())), preferred_element_type=jnp.float32
    )


def local(arriving, norm_gain, w_query, w_key, w_value, w_out):
    local_block = arriving[0]
    gain_row = norm_gain[0].astype(jnp.float32)
    query_weights = w_query[0]
    key_weights = w_key[0]
    value_weights = w_value[0]
    out_weights = w_out[0]
    mp_count = lax.axis_size(MP)
    member = lax.axis_index(MP)
    length = local_block.shape[0]
    row_count = length // mp_count
    arrived = shifted(local_block, "section", 1)
    whole_rows = lax.all_gather(arrived, MP, axis=1, tiled=True)
    full_float, normed_all = normalize(whole_rows, gain_row)
    residual = lax.dynamic_slice_in_dim(full_float, member * row_count, row_count, 0)
    projected = jnp.concatenate(
        [
            channel_product(query_weights, normed_all),
            channel_product(key_weights, normed_all),
            channel_product(value_weights, normed_all),
        ],
        axis=0,
    )
    q_width = query_weights.shape[0]
    k_width = key_weights.shape[0]
    query_pairs = jnp.arange(q_width // 2, dtype=jnp.int32) * 2 % HD // 2
    query_part = rotate_pairs(projected[:q_width], query_pairs).astype(jnp.bfloat16)
    key_pairs = (member * k_width + jnp.arange(k_width // 2, dtype=jnp.int32) * 2) // (2 * KV_HEADS)
    key_part = rotate_pairs(projected[q_width : q_width + k_width], key_pairs).astype(jnp.bfloat16)
    value_part = projected[q_width + k_width :].astype(jnp.bfloat16)
    key_all, value_all = sent_together((key_part, value_part), MP, 0, 1)
    local_heads = q_width // HD
    group_size = local_heads * mp_count // KV_HEADS
    kv_index = member * local_heads // group_size
    key_head = head_rows(key_all, kv_index)
    value_head = head_rows(value_all, kv_index)
    query_heads = query_part.reshape(local_heads, HD, length)
    score_scale = 1.0 / math.sqrt(HD)
    scores = (
        jnp.einsum("hdi,dj->hij", query_heads, key_head, preferred_element_type=jnp.float32)
        * score_scale
    )
    token_index = jnp.arange(length, dtype=jnp.int32)
    causal = token_index[:, None] >= token_index[None, :]
    scores = jnp.where(causal[None], scores, -1e30)
    row_max = jnp.max(scores, axis=-1, keepdims=True)
    exponent = jnp.exp(scores - row_max)
    row_total = jnp.sum(exponent, axis=-1, keepdims=True)
    weights = (exponent / row_total).astype(jnp.bfloat16)
    context = jnp.einsum(
        "hij,dj->ihd", weights, value_head, preferred_element_type=jnp.float32
    ).astype(jnp.bfloat16)
    context = context.reshape(length, q_width)
    full_term = jnp.dot(context, out_weights, preferred_element_type=jnp.float32)
    summed = scatter_axes(full_term.astype(jnp.bfloat16), MP, 0).astype(jnp.float32)
    attended = summed.astype(jnp.bfloat16)[None]
    stream_next = (residual + summed).astype(jnp.bfloat16)[None]
    return (attended, stream_next)


def solution(mesh):
    finer = Mesh(mesh.devices.reshape(mesh.shape["section"], 4, 8), ("section", "mp_0", "mp_1"))
    return jax.shard_map(
        local,
        mesh=finer,
        in_specs=(
            P("section", None, MP),
            P("section", None),
            P("section", MP, None),
            P("section", MP, None),
            P("section", MP, None),
            P("section", MP, None),
        ),
        out_specs=(P("section", MP, None), P("section", MP, None)),
        check_vma=False,
    )
```

profile of v0, /device:TPU:8, one launch (start us, length us, event | category | flops | bytes accessed | tf_op | source)
XLA Modules:
  0.0 442.4 jit_solution(10435901316648829320)
XLA Ops:
  7.2 0.0 copy-start
  7.2 0.0 all-gather.3.cloned.1.call-start
  7.2 0.0 collective-permute-start
  7.3 7.4 %collective-permute-done = bf16[768,256]{1,0:T(8,128)(2,1)S(1)} collective-permute-done((bf16[768,256]{1,0:T(8,128)(2,1)}, bf16[768,256]{1,0:T(8,128)(2,1)S(1)}, u32[]{:S(2)}, u32[]{:S(2)}) %collective-permute-start) | collective-permute-done | bytes 393248 | tf_op jit(solution)/shard_map/ppermute | solution.py:21
  14.7 0.0 copy-start.5
  14.7 0.7 copy-done.5
  15.4 0.0 all-gather.3.cloned.1.call-update
  15.4 0.0 all-gather.5.cloned.1.call-start
  15.5 0.8 mul.219
  16.3 127.5 %all-gather.3.cloned.1.call-done = bf16[768,8192]{1,0:T(8,128)(2,1)} async-done(((bf16[768,256]{1,0:T(8,128)(2,1)}), bf16[768,8192]{1,0:T(8,128)(2,1)}) %all-gather.3.cloned.1.call-update) | async-done | bytes 12582928 | tf_op jit(solution)/shard_map/all_gather | solution.py:92
  143.8 7.1 %multiply_reduce_fusion = f32[768]{0:T(1024)S(1)} fusion(bf16[768,8192]{1,0:T(8,128)(2,1)} %all-gather.3.cloned.1.call-done), kind=kLoop, calls=%fused_computation.2 | loop fusion | flops 18873600 | bytes 12585984 | tf_op jit(solution)/shard_map/reduce_sum | solution.py:69
  150.9 7.5 %multiply_convert_fusion = bf16[768,8192]{1,0:T(8,128)(2,1)S(1)} fusion(f32[8192]{0:T(1024)S(1)} %bitcast.54, f32[768]{0:T(1024)S(1)} %add_rsqrt_fusion, bf16[768,8192]{1,0:T(8,128)(2,1)} %all-gather.3.cloned.1.call-done), kind=kLoop, calls=%fused_computation.1 | loop fusion | flops 25165824 | bytes 25201664 | tf_op jit(solution)/shard_map/convert_element_type | solution.py:70
  158.4 0.0 copy-done
  158.4 0.0 copy-start.2
  158.4 0.0 copy-start.4
  158.4 3.8 fusion.13
  162.2 0.7 copy-done.2
  162.9 0.0 copy-done.4
  162.9 3.8 convolution_bitcast_fusion
  166.7 0.1 reshape.281
  166.8 0.1 fusion.47
  166.9 0.3 fusion.39
  167.2 0.6 pad_maximum_fusion.1
  167.9 0.0 all-gather.5.cloned.1.call-update
  167.9 0.0 reduce-scatter.3.cloned.1.call-start
  168.0 0.2 iota_compare_fusion
  168.2 14.0 %fusion.9 = f32[256,768]{1,0:T(8,128)S(1)} fusion(bf16[768,8192]{1,0:T(8,128)(2,1)} %copy-done.2, bf16[1,256,8192]{2,1,0:T(8,128)(2,1)} %param.8), kind=kOutput, calls=%fused_computation.16 | convolution fusion | flops 3221225472 | bytes 17563648 | tf_op jit(solution)/shard_map/dot_general | solution.py:75
  182.2 0.5 reshape.284
  182.7 0.6 fusion.46
  183.3 1.7 fusion.23
  185.0 0.4 copy.21
  185.4 0.1 convert_element_type.92
  185.6 59.1 %all-gather.5.cloned.1.call-done = bf16[1024,1536]{1,0:T(8,128)(2,1)} async-done(((bf16[32,1536]{1,0:T(8,128)(2,1)}), bf16[1024,1536]{1,0:T(8,128)(2,1)}) %all-gather.5.cloned.1.call-update) | async-done | bytes 3145744 | tf_op jit(solution)/shard_map/all_gather | solution.py:26
  244.7 3.2 fusion.45
  247.9 4.5 %reshape.285 = bf16[64,8,2,768]{3,2,1,0:T(2,128)(2,1)} reshape(bf16[1024,768]{1,0:T(8,128)(2,1)} %get-tuple-element.2) | data formatting | bytes 3145728 | tf_op jit(solution)/shard_map/reshape | solution.py:62
  252.4 1.1 dynamic-slice_bitcast_fusion
  253.4 0.1 reshape.286
  253.5 1.5 reshape.282
  255.1 1.1 constant_dynamic-slice_fusion
  256.1 0.1 reshape.290
  256.2 3.8 fusion.48
  260.0 0.0 copy-start.3
  260.0 3.0 fusion.12
  263.0 0.6 copy-done.3
  263.7 6.4 %convolution_convert_fusion = bf16[768,8192]{1,0:T(8,128)(2,1)} fusion(bf16[768,256]{0,1:T(8,128)(2,1)S(1)} %bitcast.53, bf16[1,256,8192]{2,1,0:T(8,128)(2,1)S(1)} %copy-done.3), kind=kOutput, calls=%fused_computation.3 | convolution fusion | flops 3227516928 | bytes 17170432 | tf_op jit(solution)/shard_map/dot_general | solution.py:133
  270.1 0.0 reduce-scatter.3.cloned.1.call-update
  270.1 0.0 reduce-scatter.5.cloned.1.call-start
  270.1 113.8 %reduce-scatter.3.cloned.1.call-done = bf16[192,8192]{1,0:T(8,128)(2,1)} async-done(((bf16[768,8192]{1,0:T(8,128)(2,1)}), bf16[192,8192]{1,0:T(8,128)(2,1)}) %reduce-scatter.3.cloned.1.call-update) | async-done | bytes 3145744 | tf_op jit(solution)/shard_map/reduce_scatter | solution.py:35
  384.0 0.0 reduce-scatter.5.cloned.1.call-update
  384.0 0.0 copy-start.1
  384.0 14.2 %convert_element_type.84 = f32[768,8192]{1,0:T(8,128)} convert(bf16[768,8192]{1,0:T(8,128)(2,1)} %all-gather.3.cloned.1.call-done) | non-fusion elementwise | flops 6291456 | bytes 37748736 | tf_op jit(solution)/shard_map/convert_element_type | solution.py:68
  398.2 35.6 %reduce-scatter.5.cloned.1.call-done = bf16[24,8192]{1,0:T(8,128)(2,1)} async-done(((bf16[192,8192]{1,0:T(8,128)(2,1)}), bf16[24,8192]{1,0:T(8,128)(2,1)}) %reduce-scatter.5.cloned.1.call-update) | async-done | bytes 393232 | tf_op jit(solution)/shard_map/reduce_scatter | solution.py:35
  433.8 2.1 fusion.26
  435.9 0.0 copy-done.1
  (8 shorter events, 0.2 us)
Async XLA Ops:
  7.2 151.2 %copy-start = (bf16[1,32,8192]{2,1,0:T(8,128)(2,1)S(1)}, bf16[1,32,8192]{2,1,0:T(8,128)(2,1)}, u32[]{:S(2)}) copy-start(bf16[1,32,8192]{2,1,0:T(8,128)(2,1)} %param.10) | copy-start | bytes 1572868
  7.2 136.6 %all-gather.3.cloned.1.call-start = ((), (), s32[]{:S(2)}) async-start(), calls=%async_computation.2 | async-start | bytes 12976128 | tf_op jit(solution)/shard_map/all_gather | solution.py:92
  7.2 7.4 %collective-permute-start = (bf16[768,256]{1,0:T(8,128)(2,1)}, bf16[768,256]{1,0:T(8,128)(2,1)S(1)}, u32[]{:S(2)}, u32[]{:S(2)}) collective-permute-start(bf16[768,256]{1,0:T(8,128)(2,1)} %bitcast.55), channel_id=1, source_target_pairs={{224,0},{0,32},{32,64},{64,96},{96,128},{128,160},{160,192},{192,2... | collective-permute-start | bytes 1179656 | tf_op jit(solution)/shard_map/ppermute | solution.py:21
  14.7 0.7 copy-start.5
  15.4 229.2 %all-gather.5.cloned.1.call-start = ((), (), s32[]{:S(2)}) async-start(), calls=%async_computation.3 | async-start | bytes 3244032 | tf_op jit(solution)/shard_map/all_gather | solution.py:26
  158.4 4.5 %copy-start.2 = (bf16[768,8192]{1,0:T(8,128)(2,1)}, bf16[768,8192]{1,0:T(8,128)(2,1)S(1)}, u32[]{:S(2)}) copy-start(bf16[768,8192]{1,0:T(8,128)(2,1)S(1)} %multiply_convert_fusion) | copy-start | bytes 37748740
  158.4 4.5 %copy-start.4 = (bf16[1,32,8192]{2,1,0:T(8,128)(2,1)S(1)}, bf16[1,32,8192]{2,1,0:T(8,128)(2,1)}, u32[]{:S(2)}) copy-start(bf16[1,32,8192]{2,1,0:T(8,128)(2,1)} %param.9) | copy-start | bytes 1572868
  167.9 216.0 %reduce-scatter.3.cloned.1.call-start = ((), (), s32[]{:S(2)}) async-start(), calls=%async_computation.4 | async-start | bytes 15728640 | tf_op jit(solution)/shard_map/reduce_scatter | solution.py:35
  260.0 3.6 copy-start.3
  270.1 163.7 %reduce-scatter.5.cloned.1.call-start = ((), (), s32[]{:S(2)}) async-start(), calls=%async_computation.5 | async-start | bytes 3538944 | tf_op jit(solution)/shard_map/reduce_scatter | solution.py:35
  384.0 51.9 %copy-start.1 = (bf16[1,32,8192]{2,1,0:T(8,128)(2,1)S(1)}, bf16[1,32,8192]{2,1,0:T(8,128)(2,1)}, u32[]{:S(2)}) copy-start(bf16[1,32,8192]{2,1,0:T(8,128)(2,1)} %param.10) | copy-start | bytes 1572868
Sparse Core Ops, SparseCore 0:
  15.5 128.1 all-gather.2
  168.0 76.5 all-gather.4
  270.2 113.6 reduce-scatter.2
  386.9 46.8 reduce-scatter.4
where the time goes:
time: 443 us; the launch traced here: 442 us
  waiting for transfers between devices  343 us (77%)
  matrix products  34.9 us (8%)
  other arithmetic  34.5 us (8%)
  local copies, waits for them, and re-layouts  15.5 us (3%)
  between operations  14 us (3%)
    reduce_scatter x2, waiting for transfers between devices, scatter_axes(): array = lax.psum_scatter(array, axis, scatter_dimension=dim, tiled=True)  149 us
    all_gather x1, waiting for transfers between devices, local(): whole_rows = lax.all_gather(arrived, MP, axis=1, tiled=True)  127 us
    all_gather x1, waiting for transfers between devices, sent_together(): result, at, outs = (lax.all_gather(both, axis, axis=dim, tiled=True), 0, [])  59.1 us
    dot_general x3, matrix products, channel_product(): lax.dot_general(weights, normed, (((1,), (1,)), ((), ())), preferred_elem...  21.7 us
    convert_element_type x1, other arithmetic, normalize(): as_float = hidden_in.astype(jnp.float32)  14.2 us
  transfers between devices with their start and end apart: 5, of which 5 were waited for; matrix products, arithmetic and copies ran while one was open for 7% of the time, Pallas kernels for 0%

commit v1 on v0

v1 whole, which is shorter than its diff:
```python
import functools
import math

import jax
import jax.numpy as jnp
from jax import lax
from jax.experimental import pallas as pl
from jax.experimental.pallas import tpu as pltpu
from jax.sharding import PartitionSpec as P

MESH = pl.DeviceIdType.MESH
BF16 = jnp.bfloat16
F32 = jnp.float32

X = 4
Z = 8
N = X * Z
SECTIONS = 8
LENGTH = 768
D = 8192
HD = 128
KV_HEADS = 8
WIDTH = D // N
ROWS = LENGTH // N
STREAMS = 4
QUARTER = LENGTH // STREAMS
PIECES = 4
PIECE = QUARTER // PIECES
SUMS = ROWS * D // 128 // STREAMS
SUM = SUMS // PIECES
QB = 256

ROPE_BASE = 500000.0
EPS = 1e-05


def spot(cycle, m):
    x, z = m // Z, lax.rem(m, Z)
    if cycle == 0:
        return X * z + lax.rem(x + z, X)
    b = lax.rem(z - 3 * x + 2 * Z, Z)
    return 4 * (x + X * (b // 4)) + lax.rem(b, 4)


def member(cycle, i):
    i = lax.rem(i, N)
    a, b = i // 4, lax.rem(i, 4)
    if cycle == 0:
        x, z = lax.rem(b - a + N, X), a
    else:
        x, z = lax.rem(a, X), lax.rem(3 * a + b, Z)
    return x * Z + z


def kernel(
    arriving, gain, w_query, w_key, w_value, w_out, cos_q, sin_q, turn_kv,
    attended, stream,
    hidden, wq, wkv_raw, wkv, wo, acc, squares, q_rot, own_kv, column_kv, all_kv, keys, values, context, term, landed,
    w_sem, shift_send, shift_recv, gather_send, gather_recv, x_send, x_recv, z_send, z_recv, scatter_send, scatter_recv,
):
    me = lax.axis_index("mp")
    section = lax.axis_index("section")
    x, z = me // Z, lax.rem(me, Z)
    cycles = [0, 0, 1, 1]
    forward = [True, False, True, False]
    places = [spot(c, me) for c in cycles]
    nexts = [
        member(c, p + (1 if f else N - 1)) for c, p, f in zip(cycles, places, forward)
    ]

    def behind(s, k):
        return member(cycles[s], places[s] + (N - k if forward[s] else k))

    loads = [
        pltpu.make_async_copy(w_key.at[0], wkv_raw.at[0], w_sem.at[0]),
        pltpu.make_async_copy(w_value.at[0], wkv_raw.at[1], w_sem.at[1]),
        pltpu.make_async_copy(w_query.at[0], wq, w_sem.at[2]),
        pltpu.make_async_copy(w_out.at[0], wo, w_sem.at[3]),
    ]
    for load in loads:
        load.start()

    barrier = pltpu.get_barrier_semaphore()
    for step in range(1, X):
        pl.semaphore_signal(
            barrier, inc=1, device_id={"mp": lax.rem(x + step, X) * Z + z}, device_id_type=MESH
        )
    for step in range(1, Z):
        pl.semaphore_signal(
            barrier, inc=1, device_id={"mp": x * Z + lax.rem(z + step, Z)}, device_id_type=MESH
        )
    for step in (1, SECTIONS - 1):
        pl.semaphore_signal(
            barrier, inc=1, device_id={"section": lax.rem(section + step, SECTIONS)}, device_id_type=MESH
        )
    pl.semaphore_wait(barrier, (X - 1) + (Z - 1) + 2)

    shifts = []
    for s in range(STREAMS):
        rows = pl.ds(s * QUARTER, QUARTER)
        shifts.append(
            pltpu.make_async_remote_copy(
                src_ref=arriving.at[0, rows],
                dst_ref=hidden.at[me, rows],
                send_sem=shift_send.at[s],
                recv_sem=shift_recv.at[s],
                device_id={"section": lax.rem(section + 1, SECTIONS)},
                device_id_type=MESH,
            )
        )
        shifts[-1].start()

    def pass_on(s, c, k, owner):
        part = hidden.at[owner, pl.ds(s * QUARTER + c * PIECE, PIECE)]
        return pltpu.make_async_remote_copy(
            src_ref=part,
            dst_ref=part,
            send_sem=gather_send.at[lax.rem(k, 2), s, c],
            recv_sem=gather_recv.at[k, s, c],
            device_id={"mp": nexts[s]},
            device_id_type=MESH,
        )

    def project(s, owner, first=False):
        rows = pl.ds(s * QUARTER, QUARTER)
        columns = pl.ds(pl.multiple_of(owner * WIDTH, WIDTH), WIDTH)
        block = hidden[owner, rows].astype(F32)
        squared = block * block
        squared = squared[:, :128] + squared[:, 128:]
        scaled = (block * gain[:, columns].astype(F32)).astype(BF16)
        contract = (((1,), (1,)), ((), ()))
        queries = lax.dot_general(scaled, wq[:, columns], contract, preferred_element_type=F32)
        others = lax.dot_general(scaled, wkv[:, columns], contract, preferred_element_type=F32)
        if first:
            squares[rows] = squared
            acc[rows, :WIDTH] = queries
            acc[rows, WIDTH:] = others
        else:
            squares[rows] += squared
            acc[rows, :WIDTH] += queries
            acc[rows, WIDTH:] += others

    for s in range(STREAMS):
        shifts[s].wait_recv()
        for c in range(PIECES):
            pass_on(s, c, 0, me).start()

    loads[0].wait()
    loads[1].wait()
    out_row = lax.broadcasted_iota(jnp.int32, (128, 64), 0)
    raw_row = lax.broadcasted_iota(jnp.int32, (128, 64), 1)
    head, j = lax.rem(out_row, 64) // 8, lax.rem(out_row, 8)
    channel = lax.rem(j, 4)
    turned = jnp.where(out_row >= 64, channel + 1 - 2 * lax.rem(channel, 2), channel)
    source = (j // 4) * 32 + (turned // 2) * 16 + head * 2 + lax.rem(turned, 2)
    pick = (raw_row == source).astype(F32).astype(BF16)
    for part in range(8):
        columns = pl.ds(part * (D // 8), D // 8)
        raw = jnp.concatenate([wkv_raw[0, :, columns], wkv_raw[1, :, columns]], axis=0)
        wkv[:, columns] = jnp.dot(pick, raw, preferred_element_type=F32).astype(BF16)
    loads[2].wait()
    for s in range(STREAMS):
        project(s, me, first=True)

    def gather_step(k, carry):
        for c in range(PIECES):
            for s in range(STREAMS):
                pass_on(s, c, k, behind(s, k + 1)).wait_recv()

                @pl.when(k >= 1)
                def _():
                    pass_on(s, c, k + 1, me).wait_send()

                pass_on(s, c, k + 1, behind(s, k + 1)).start()

            @pl.when(k >= 1)
            def _():
                project(c, behind(c, k))

        return carry

    lax.fori_loop(0, N - 2, gather_step, 0)
    for s in range(STREAMS):
        project(s, behind(s, N - 2))
    for s in range(STREAMS):
        for c in range(PIECES):
            pass_on(s, c, N - 2, behind(s, N - 1)).wait_recv()
        project(s, behind(s, N - 1))
    for s in range(STREAMS):
        for c in range(PIECES):
            pass_on(s, c, N - 3, me).wait_send()
            pass_on(s, c, N - 2, me).wait_send()
        shifts[s].wait_send()

    def scale_of(rows):
        mean = jnp.sum(squares[rows], axis=1, keepdims=True) * (1.0 / D)
        return lax.rsqrt(mean + EPS)

    for t in range(3):
        rows = pl.ds(t * QB, QB)
        both = acc[rows, WIDTH:] * scale_of(rows) * turn_kv[rows]
        ready = (both + pltpu.roll(both, 64, 1)).T
        for h in range(KV_HEADS):
            tile = ready[8 * h : 8 * h + 8]
            own_kv[h, t] = jnp.concatenate([tile[:, :128], tile[:, 128:]], axis=0).astype(BF16)

    x_copies = []
    for step in range(1, X):
        to = lax.rem(x + step, X)
        x_copies.append(
            pltpu.make_async_remote_copy(
                src_ref=own_kv.at[pl.ds(2 * to, 2)],
                dst_ref=column_kv.at[x],
                send_sem=x_send.at[step - 1],
                recv_sem=x_recv.at[step - 1],
                device_id={"mp": to * Z + z},
                device_id_type=MESH,
            )
        )
        x_copies[-1].start()
    for h in range(2):
        column_kv[x, h] = own_kv[2 * x + h]
    for copy in x_copies:
        copy.wait_recv()
    z_copies = []
    for step in range(1, Z):
        to = lax.rem(z + step, Z)
        z_copies.append(
            pltpu.make_async_remote_copy(
                src_ref=column_kv.at[:, to // 4],
                dst_ref=all_kv.at[:, z],
                send_sem=z_send.at[step - 1],
                recv_sem=z_recv.at[step - 1],
                device_id={"mp": x * Z + to},
                device_id_type=MESH,
            )
        )
        z_copies[-1].start()
    all_kv[:, z] = column_kv[:, z // 4]

    lane = lax.broadcasted_iota(jnp.int32, (QB, HD), 1)
    even = lax.rem(lane, 2) == 0
    for t in range(3):
        rows = pl.ds(t * QB, QB)
        scale = scale_of(rows)
        for h in range(2):
            query = acc[rows, h * HD : (h + 1) * HD] * scale
            swapped = jnp.where(even, pltpu.roll(query, HD - 1, 1), pltpu.roll(query, 1, 1))
            rotated = query * cos_q[rows] + swapped * sin_q[rows]
            q_rot[rows, h * HD : (h + 1) * HD] = rotated.astype(BF16)

    for copy in x_copies:
        copy.wait_send()
    for copy in z_copies:
        copy.wait()

    want = lax.broadcasted_iota(jnp.int32, (512, 512), 0)
    have = lax.broadcasted_iota(jnp.int32, (512, 512), 1)
    channel = lax.rem(want, 128)
    source = 16 * (channel // 4) + 4 * (want // 128) + lax.rem(channel, 4)
    pick = (have == source).astype(F32).astype(BF16)
    for t in range(3):
        arrived = all_kv[:, :, t].reshape(512, 128)
        sorted_rows = jnp.dot(pick, arrived, preferred_element_type=F32).astype(BF16)
        for half in range(2):
            columns = slice(t * QB + half * 128, t * QB + half * 128 + 128)
            keys[:, columns] = sorted_rows[256 * half : 256 * half + 128]
            values[:, columns] = sorted_rows[256 * half + 128 : 256 * half + 256]

    for t in range(3):
        rows = slice(t * QB, (t + 1) * QB)
        reach = (t + 1) * QB
        token = lax.broadcasted_iota(jnp.int32, (QB, reach), 0) + t * QB
        causal = token >= lax.broadcasted_iota(jnp.int32, (QB, reach), 1)
        for h in range(2):
            scores = jnp.dot(
                q_rot[rows, h * HD : (h + 1) * HD], keys[:, :reach], preferred_element_type=F32
            ) * (1.0 / math.sqrt(HD))
            scores = jnp.where(causal, scores, -1e30)
            exponent = jnp.exp(scores - jnp.max(scores, axis=1, keepdims=True))
            probs = (exponent / jnp.sum(exponent, axis=1, keepdims=True)).astype(BF16)
            mixed = lax.dot_general(
                probs, values[:, :reach], (((1,), (1,)), ((), ())), preferred_element_type=F32
            )
            context[rows, h * HD : (h + 1) * HD] = mixed.astype(BF16)

    def hand_on(s, c, k, owner):
        rows = pl.ds(s * SUMS + c * SUM, SUM)
        return pltpu.make_async_remote_copy(
            src_ref=term.at[owner, rows],
            dst_ref=landed.at[k, rows],
            send_sem=scatter_send.at[lax.rem(k, 2), s, c],
            recv_sem=scatter_recv.at[k, s, c],
            device_id={"mp": nexts[s]},
            device_id_type=MESH,
        )

    loads[3].wait()

    def project_out(tile):
        columns = pl.ds(pl.multiple_of(tile * 256, 256), 256)
        rows = pl.ds(pl.multiple_of(tile * 2 * ROWS, 2 * ROWS), 2 * ROWS)
        product = jnp.dot(context[...], wo[:, columns], preferred_element_type=F32)
        for owner in range(N):
            mine = product[owner * ROWS : (owner + 1) * ROWS]
            term[owner, rows] = jnp.concatenate([mine[:, :128], mine[:, 128:]], axis=0).astype(BF16)

    tiles = SUM // (2 * ROWS)
    for c in range(PIECES):

        def some(i, carry):
            s, u = i // tiles, lax.rem(i, tiles)
            project_out(s * (SUMS // (2 * ROWS)) + c * tiles + u)
            return carry

        lax.fori_loop(0, STREAMS * tiles, some, 0)
        for s in range(STREAMS):
            hand_on(s, c, 0, behind(s, 1)).start()

    def scatter_step(k, carry):
        for c in range(PIECES):
            for s in range(STREAMS):
                owner = behind(s, k + 2)
                rows = pl.ds(s * SUMS + c * SUM, SUM)
                hand_on(s, c, k, owner).wait_recv()

                @pl.when(k >= 1)
                def _():
                    hand_on(s, c, k + 1, owner).wait_send()

                total = term[owner, rows].astype(F32) + landed[k, rows].astype(F32)
                term[owner, rows] = total.astype(BF16)
                hand_on(s, c, k + 1, owner).start()
        return carry

    lax.fori_loop(0, N - 2, scatter_step, 0)

    first = me * ROWS
    offset = lax.rem(me, 2) * 8
    window = pl.ds(pl.multiple_of(first - offset, 16), ROWS + 8)

    for s in range(STREAMS):
        for c in range(PIECES):
            hand_on(s, c, N - 2, me).wait_recv()
            for u in range(tiles):
                at = s * SUMS + c * SUM + u * 2 * ROWS
                total = term[me, at : at + 2 * ROWS].astype(F32) + landed[N - 2, at : at + 2 * ROWS].astype(F32)
                owner = at // (2 * ROWS)
                total = jnp.concatenate([total[:ROWS], total[ROWS:]], axis=1)
                wide = hidden[owner, window].astype(F32)
                residual = jnp.where(offset == 0, wide[:ROWS], wide[8:])
                columns = slice(owner * WIDTH, (owner + 1) * WIDTH)
                attended[0, :, columns] = total.astype(BF16)
                stream[0, :, columns] = (residual + total).astype(BF16)
    for s in range(STREAMS):
        for c in range(PIECES):
            hand_on(s, c, N - 3, me).wait_send()
            hand_on(s, c, N - 2, me).wait_send()


def tables():
    member_id = lax.axis_index("mp")
    lanes = jnp.arange(HD, dtype=jnp.int32)
    positions = jnp.arange(LENGTH, dtype=jnp.int32).astype(F32)

    def angles(pairs):
        frequency = jnp.exp(pairs.astype(F32) * (-2.0 * math.log(ROPE_BASE) / HD))
        return positions[:, None] * frequency[None, :]

    sign = jnp.where(lanes % 2 == 0, -1.0, 1.0)
    turn = angles(lanes // 2)
    cos_q, sin_q = jnp.cos(turn), jnp.sin(turn) * sign
    j = lanes % 8
    turn = angles(2 * member_id + (j % 4) // 2)
    key_lane = j < 4
    turn_kv = jnp.where(
        lanes[None, :] < 64,
        jnp.where(key_lane, jnp.cos(turn), 1.0),
        jnp.where(key_lane, jnp.sin(turn) * sign, 0.0),
    )
    return cos_q, sin_q, turn_kv


def layer(arriving, norm_gain, w_query, w_key, w_value, w_out):
    any_space = pl.BlockSpec(memory_space=pl.ANY)
    vmem = pl.BlockSpec(memory_space=pltpu.VMEM)
    out = jax.ShapeDtypeStruct((1, ROWS, D), BF16)
    dma = pltpu.SemaphoreType.DMA
    return pl.pallas_call(
        kernel,
        out_shape=(out, out),
        in_specs=[vmem, vmem, any_space, any_space, any_space, any_space, vmem, vmem, vmem],
        out_specs=(vmem, vmem),
        scratch_shapes=[
            pltpu.VMEM((N, LENGTH, WIDTH), BF16),
            pltpu.VMEM((WIDTH, D), BF16),
            pltpu.VMEM((2, 32, D), BF16),
            pltpu.VMEM((128, D), BF16),
            pltpu.VMEM((WIDTH, D), BF16),
            pltpu.VMEM((LENGTH, WIDTH + 128), F32),
            pltpu.VMEM((LENGTH, 128), F32),
            pltpu.VMEM((LENGTH, WIDTH), BF16),
            pltpu.VMEM((KV_HEADS, 3, 16, 128), BF16),
            pltpu.VMEM((X, 2, 3, 16, 128), BF16),
            pltpu.VMEM((X, Z, 3, 16, 128), BF16),
            pltpu.VMEM((HD, LENGTH), BF16),
            pltpu.VMEM((HD, LENGTH), BF16),
            pltpu.VMEM((LENGTH, WIDTH), BF16),
            pltpu.VMEM((N, STREAMS * SUMS, 128), BF16),
            pltpu.VMEM((N - 1, STREAMS * SUMS, 128), BF16),
            dma((4,)),
            dma((STREAMS,)),
            dma((STREAMS,)),
            dma((2, STREAMS, PIECES)),
            dma((N - 1, STREAMS, PIECES)),
            dma((X - 1,)),
            dma((X - 1,)),
            dma((Z - 1,)),
            dma((Z - 1,)),
            dma((2, STREAMS, PIECES)),
            dma((N - 1, STREAMS, PIECES)),
        ],
        compiler_params=pltpu.CompilerParams(
            collective_id=0, has_side_effects=True, vmem_limit_bytes=67043328
        ),
    )(arriving, norm_gain, w_query, w_key, w_value, w_out, *tables())


def solution(mesh):
    return jax.shard_map(
        layer,
        mesh=mesh,
        in_specs=(
            P("section", None, "mp"),
            P("section", None),
            P("section", "mp", None),
            P("section", "mp", None),
            P("section", "mp", None),
            P("section", "mp", None),
        ),
        out_specs=(P("section", "mp", None), P("section", "mp", None)),
        check_vma=False,
    )
```

time: 443 us -> 278 us (0.63)
  waiting for transfers between devices: 343 us -> 0 us
  Pallas kernels: 0 us -> 267 us
  matrix products: 34.9 us -> 0 us
  other arithmetic: 34.5 us -> 4.19 us
  between operations: 14 us -> 0.67 us
  local copies, waits for them, and re-layouts: 15.5 us -> 3.53 us
    pallas_call x0 -> x1, Pallas kernels: none -> 267 us  [layer(): pl.pallas_call(kernel, out_shape=(out, out), in_specs=[vmem, vmem, any_sp...]
    all_gather x2 -> x0, waiting for transfers between devices: 187 us -> none  [the longest x1 127 us: local(): whole_rows = lax.all_gather(arrived, MP, axis=1, tiled=True)]
    reduce_scatter x2 -> x0, waiting for transfers between devices: 149 us -> none  [scatter_axes(): array = lax.psum_scatter(array, axis, scatter_dimension=dim, tiled=True)]
    dot_general x5 -> x0, matrix products: 31.1 us -> none  [the longest x3 21.7 us: channel_product(): lax.dot_general(weights, normed, (((1,), (1,)), ((), ())), preferred_elem...]
    convert_element_type x3 -> x1, other arithmetic: 21.7 us -> 0.01 us  [tables(): positions = jnp.arange(LENGTH, dtype=jnp.int32).astype(F32)]
    ppermute x1 -> x0, waiting for transfers between devices: 7.4 us -> none  [shifted(): return lax.ppermute(block, axis, route)]
    reduce_sum x1 -> x0, other arithmetic: 7.09 us -> none  [normalize(): mean_square = jnp.mean(as_float * as_float, axis=1, keepdims=True)]
    reshape x6 -> x0, local copies, waits for them, and re-layouts: 6.72 us -> none  [the longest x2 6.04 us: head_rows(): grouped = table.reshape(HD // 2, KV_HEADS, 2, length)]
  transfers between devices with their start and end apart: 5 -> 0, of which waited for: 5 -> 0; matrix products, arithmetic and copies ran while one was open for 7% -> 0% of each run, Pallas kernels for 0% -> 0%
where the time goes in v1:
time: 278 us; the launch traced here: 276 us
  Pallas kernels  267 us (96%)
  other arithmetic  4.19 us (2%)
  local copies, waits for them, and re-layouts  3.53 us (1%)
    pallas_call x1, Pallas kernels, layer(): pl.pallas_call(kernel, out_shape=(out, out), in_specs=[vmem, vmem, any_sp...  267 us

profile of v1, /device:TPU:8, one launch (start us, length us, event | category | flops | bytes accessed | tf_op | source)
XLA Modules:
  0.0 275.5 jit_solution(681837104431157257)
XLA Ops:
  0.7 4.2 %fusion.2 = (f32[768,128]{1,0:T(8,128)}, f32[768,128]{1,0:T(8,128)}, f32[768,128]{1,0:T(8,128)}) fusion(f32[128]{0:T(128)S(1)} %multiply_exponential_fusion, f32[128]{0:T(128)S(1)} %get-tuple-element.5, f32[768]{0:T(1024)S(1)} %iota_convert_fusion, pred[128]{0:T(512)(128)(4,1)S(1)} %get-tuple-element.8, pred[128]{0:T(512)(128)(4,1)S(1)} %get-tuple-element.7, ...), kind=kLoop, calls=%fused_computation.6 | loop fusion | flops 688128 | bytes 1184512 | tf_op jit(solution)/shard_map/jit(_where)/select_n | solution.py:376
  4.8 267.1 %shard_map.77 = (bf16[1,24,8192]{2,1,0:T(8,128)(2,1)}, bf16[1,24,8192]{2,1,0:T(8,128)(2,1)}) custom-call(bf16[1,768,256]{2,1,0:T(8,128)(2,1)} %arriving.1, bf16[1,8192]{1,0:T(2,128)(2,1)} %gain.1, bf16[1,256,8192]{2,1,0:T(8,128)(2,1)} %w_query.1, bf16[1,32,8192]{2,1,0:T(8,128)(2,1)} %w_key.1, bf16[1,32,8192]{2,1,0:T(8,128)(2,1)} %w_value.1, ...), custom_call_target="tpu_custom_call" | custom-call | tf_op jit(solution)/shard_map/pallas_call | solution.py:389
  272.0 1.8 copy.10
  273.8 1.8 copy.11
  (4 shorter events, 0.0 us)

commit v2 on v1

v2 whole, which is shorter than its diff:
```python
import math

import jax
import jax.numpy as jnp
from jax import lax
from jax.experimental import pallas as pl
from jax.experimental.pallas import tpu as pltpu
from jax.sharding import PartitionSpec as P

MESH = pl.DeviceIdType.MESH
BF16 = jnp.bfloat16
F32 = jnp.float32

X = 4
Z = 8
N = X * Z
SECTIONS = 8
LENGTH = 768
D = 8192
HD = 128
KV_HEADS = 8
WIDTH = D // N
ROWS = LENGTH // N
UNIT = 2 * ROWS
QB = 256

ROPE_BASE = 500000.0
EPS = 1e-05

LINKS = ("x+", "x-", "z+", "z-")
STEP = {"x+": (1, 0), "x-": (-1, 0), "z+": (0, 1), "z-": (0, -1)}
OPPOSITE = {"x+": "x-", "x-": "x+", "z+": "z-", "z-": "z+"}
GATHER_CUTS = (0, 160, 320, 544, 768)
SCATTER_CUTS = (0, 6, 13, 23, 32)


def plan(cuts):
    a0, a1, a2, b1, b2 = cuts
    copies = {}
    for sign in (1, -1):
        x_link, z_link = ("x+", "z+") if sign == 1 else ("x-", "z-")
        half_a = (a0, a1) if sign == 1 else (a1, a2)
        half_b = (a2, b1) if sign == 1 else (b1, b2)
        copies[x_link, "A", 0] = ((), (a0, a2), (0, 0))
        copies[x_link, "A", 1] = (((x_link, "A", 0),), half_a, (-sign, 0))
        for o in (0, -1, 1, -2, 2, -3, 3, 4):
            if o == 0:
                wanted = ()
            elif o == 4:
                wanted = (("z+", "B", 3), ("z-", "B", 3))
            else:
                wanted = (("z+" if o < 0 else "z-", "B", abs(o) - 1),)
            copies[x_link, "B", o] = (wanted, (a2, b2), (0, o))
            copies[x_link, "C", o] = (((x_link, "B", o),), half_b, (-sign, o))
        for hop in range(4):
            wanted = ((z_link, "B", hop - 1),) if hop else ()
            copies[z_link, "B", hop] = (wanted, half_b if hop == 3 else (a2, b2), (0, -sign * hop))
        for i in (0, -1, 1, 2):
            first = {0: (), -1: (("x+", "A", 0),), 1: (("x-", "A", 0),), 2: (("x+", "A", 1), ("x-", "A", 1))}[i]
            for hop in range(4):
                wanted = ((z_link, "A", hop - 1, i),) if hop else first
                copies[z_link, "A", hop, i] = (wanted, half_a if hop == 3 else (a0, a2), (i, -sign * hop))
    return copies


def backwards(copies):
    after = {key: [] for key in copies}
    for key, (wanted, _, _) in copies.items():
        for other in wanted:
            after[other].append(key)
    return {key: (tuple(after[key]), rows, at) for key, (_, rows, at) in copies.items()}


def in_order(copies, bytes_per_row, rate=46.6e3, latency=2.5, queue=2):
    length = {key: (rows[1] - rows[0]) * bytes_per_row / rate for key, (_, rows, _) in copies.items()}
    after = backwards(copies)
    chain = {}

    def chain_of(key):
        if key not in chain:
            chain[key] = length[key] + max([chain_of(k) for k in after[key][0]], default=0.0)
        return chain[key]

    left, ready, queued = list(copies), {link: [] for link in LINKS}, {link: [] for link in LINKS}
    free = {link: 0.0 for link in LINKS}
    arrival, start, now = {}, {}, 0.0
    while left or any(ready.values()):
        for key in list(left):
            if all(k in arrival and arrival[k] <= now + 1e-9 for k in copies[key][0]):
                left.remove(key)
                ready[key[0]].append(key)
        for link in LINKS:
            queued[link] = [t for t in queued[link] if t > now + 1e-9]
            while ready[link] and len(queued[link]) < queue:
                key = max(ready[link], key=chain_of)
                ready[link].remove(key)
                start[key] = now
                free[link] = max(now, free[link]) + length[key]
                queued[link].append(free[link])
                arrival[key] = free[link] + latency
        times = [t for t in arrival.values() if t > now + 1e-9] + [t for q in queued.values() for t in q if t > now + 1e-9]
        now = min(times, default=now)
    return start, arrival


def seen_from_receiver(key, at):
    dx, dz = STEP[key[0]]
    return (at[0] - dx) % X, (at[1] - dz) % Z


GATHER = plan(GATHER_CUTS)
SCATTER = backwards(plan(SCATTER_CUTS))
KEYS = list(GATHER)
NUMBER = {key: n for n, key in enumerate(KEYS)}
SLOT = {}
LANDED = 0
for _key in KEYS:
    SLOT[_key] = LANDED
    LANDED += (SCATTER[_key][1][1] - SCATTER[_key][1][0]) * UNIT


def kernel(
    arriving, gain, w_query, w_key, w_value, w_out,
    attended, stream,
    hidden, wq, wkv_raw, wkv, wo, acc, squares, cos_q, sin_q, turn_kv, q_rot, own_kv, column_kv, all_kv, keys, values,
    context, term, landed,
    w_sem, shift_send, shift_recv, gather_send, gather_recv, x_send, x_recv, z_send, z_recv, scatter_send, scatter_recv,
):
    me = lax.axis_index("mp")
    section = lax.axis_index("section")
    x, z = me // Z, lax.rem(me, Z)

    def near(dx, dz):
        return lax.rem(x + dx % X, X) * Z + lax.rem(z + dz % Z, Z)

    loads = [
        pltpu.make_async_copy(w_key.at[0], wkv_raw.at[0], w_sem.at[0]),
        pltpu.make_async_copy(w_value.at[0], wkv_raw.at[1], w_sem.at[1]),
        pltpu.make_async_copy(w_query.at[0], wq, w_sem.at[2]),
        pltpu.make_async_copy(w_out.at[0], wo, w_sem.at[3]),
    ]
    for load in loads:
        load.start()

    barrier = pltpu.get_barrier_semaphore()
    for step in range(1, X):
        pl.semaphore_signal(barrier, inc=1, device_id={"mp": near(step, 0)}, device_id_type=MESH)
    for step in range(1, Z):
        pl.semaphore_signal(barrier, inc=1, device_id={"mp": near(0, step)}, device_id_type=MESH)
    for step in (1, SECTIONS - 1):
        pl.semaphore_signal(
            barrier, inc=1, device_id={"section": lax.rem(section + step, SECTIONS)}, device_id_type=MESH
        )
    pl.semaphore_wait(barrier, (X - 1) + (Z - 1) + 2)

    parts = (GATHER_CUTS[0], GATHER_CUTS[2], GATHER_CUTS[4])
    shifts = []
    for s in range(2):
        rows = pl.ds(parts[s], parts[s + 1] - parts[s])
        shifts.append(
            pltpu.make_async_remote_copy(
                src_ref=arriving.at[0, rows],
                dst_ref=hidden.at[me, rows],
                send_sem=shift_send.at[s],
                recv_sem=shift_recv.at[s],
                device_id={"section": lax.rem(section + 1, SECTIONS)},
                device_id_type=MESH,
            )
        )
        shifts[-1].start()

    loads[0].wait()
    loads[1].wait()
    out_row = lax.broadcasted_iota(jnp.int32, (128, 64), 0)
    raw_row = lax.broadcasted_iota(jnp.int32, (128, 64), 1)
    head, j = lax.rem(out_row, 64) // 8, lax.rem(out_row, 8)
    channel = lax.rem(j, 4)
    turned = jnp.where(out_row >= 64, channel + 1 - 2 * lax.rem(channel, 2), channel)
    source = (j // 4) * 32 + (turned // 2) * 16 + head * 2 + lax.rem(turned, 2)
    pick = (raw_row == source).astype(F32).astype(BF16)
    for part in range(8):
        columns = pl.ds(part * (D // 8), D // 8)
        raw = jnp.concatenate([wkv_raw[0, :, columns], wkv_raw[1, :, columns]], axis=0)
        wkv[:, columns] = jnp.dot(pick, raw, preferred_element_type=F32).astype(BF16)

    def passed(key):
        _, (low, high), at = GATHER[key]
        block = hidden.at[near(*at), pl.ds(low, high - low)]
        return pltpu.make_async_remote_copy(
            src_ref=block,
            dst_ref=block,
            send_sem=gather_send.at[NUMBER[key]],
            recv_sem=gather_recv.at[NUMBER[key]],
            device_id={"mp": near(*STEP[key[0]])},
            device_id_type=MESH,
        )

    def arrived_block(key):
        _, (low, high), at = GATHER[key]
        block = hidden.at[near(*seen_from_receiver(key, at)), pl.ds(low, high - low)]
        return pltpu.make_async_remote_copy(
            src_ref=block,
            dst_ref=block,
            send_sem=gather_send.at[NUMBER[key]],
            recv_sem=gather_recv.at[NUMBER[key]],
            device_id={"mp": near(*STEP[key[0]])},
            device_id_type=MESH,
        )

    started_rows = set()

    def project(part, at):
        owner = near(*at)
        rows = pl.ds(parts[part], parts[part + 1] - parts[part])
        columns = pl.ds(pl.multiple_of(owner * WIDTH, WIDTH), WIDTH)
        block = hidden[owner, rows].astype(F32)
        squared = block * block
        squared = squared[:, :128] + squared[:, 128:]
        scaled = (block * gain[:, columns].astype(F32)).astype(BF16)
        contract = (((1,), (1,)), ((), ()))
        queries = lax.dot_general(scaled, wq[:, columns], contract, preferred_element_type=F32)
        others = lax.dot_general(scaled, wkv[:, columns], contract, preferred_element_type=F32)
        if part not in started_rows:
            started_rows.add(part)
            squares[rows] = squared
            acc[rows, :WIDTH] = queries
            acc[rows, WIDTH:] = others
        else:
            squares[rows] += squared
            acc[rows, :WIDTH] += queries
            acc[rows, WIDTH:] += others

    def rotary_table(i):
        size = 64
        rows = pl.ds(i * size, size)
        lane = lax.broadcasted_iota(jnp.int32, (size, HD), 1)
        token = (lax.broadcasted_iota(jnp.int32, (size, HD), 0) + i * size).astype(F32)
        sign = jnp.where(lax.rem(lane, 2) == 0, -1.0, 1.0)

        def angle(pair):
            return token * jnp.exp(pair.astype(F32) * (-2.0 * math.log(ROPE_BASE) / HD))

        turn = angle(lane // 2)
        cos_q[rows] = jnp.cos(turn)
        sin_q[rows] = jnp.sin(turn) * sign
        j = lax.rem(lane, 8)
        turn = angle(2 * me + lax.rem(j, 4) // 2)
        stay = jnp.where(j < 4, jnp.cos(turn), 1.0)
        cross = jnp.where(j < 4, jnp.sin(turn) * sign, 0.0)
        turn_kv[rows] = jnp.where(lane < 64, stay, cross)

    start, arrival = in_order(GATHER, 2 * WIDTH)
    bringing = {((0, 0), 0): [], ((0, 0), 1): []}
    for key, (_, (low, _), at) in GATHER.items():
        bringing.setdefault((seen_from_receiver(key, at), int(low >= parts[1])), []).append(key)
    events = [(t, 0, "pass", key) for key, t in start.items()]
    events += [
        (max([arrival[k] for k in by], default=0.0) + (1.0 if by else 0.0), 1, "project", which)
        for which, by in bringing.items()
    ]
    events += [(3.0 + 1.5 * i, 2, "table", i) for i in range(12)]
    events.sort(key=lambda event: event[:2])
    waited = set()

    def need(key):
        if key not in waited:
            waited.add(key)
            arrived_block(key).wait_recv()

    shifts[0].wait_recv()
    shifts[1].wait_recv()
    query_weights_here = False
    for _, _, what, which in events:
        if what == "pass":
            for key in GATHER[which][0]:
                need(key)
            passed(which).start()
        elif what == "project":
            if not query_weights_here:
                query_weights_here = True
                loads[2].wait()
            for key in bringing[which]:
                need(key)
            project(which[1], which[0])
        else:
            rotary_table(which)

    def scale_of(rows):
        mean = jnp.sum(squares[rows], axis=1, keepdims=True) * (1.0 / D)
        return lax.rsqrt(mean + EPS)

    for t in range(3):
        rows = pl.ds(t * QB, QB)
        both = acc[rows, WIDTH:] * scale_of(rows) * turn_kv[rows]
        ready = (both + pltpu.roll(both, 64, 1)).T
        for h in range(KV_HEADS):
            tile = ready[8 * h : 8 * h + 8]
            own_kv[h, t] = jnp.concatenate([tile[:, :128], tile[:, 128:]], axis=0).astype(BF16)

    x_copies = []
    for step in range(1, X):
        to = lax.rem(x + step, X)
        x_copies.append(
            pltpu.make_async_remote_copy(
                src_ref=own_kv.at[pl.ds(2 * to, 2)],
                dst_ref=column_kv.at[x],
                send_sem=x_send.at[step - 1],
                recv_sem=x_recv.at[step - 1],
                device_id={"mp": near(step, 0)},
                device_id_type=MESH,
            )
        )
        x_copies[-1].start()
    for h in range(2):
        column_kv[x, h] = own_kv[2 * x + h]
    for copy in x_copies:
        copy.wait_recv()
    z_copies = []
    for step in range(1, Z):
        to = lax.rem(z + step, Z)
        z_copies.append(
            pltpu.make_async_remote_copy(
                src_ref=column_kv.at[:, to // 4],
                dst_ref=all_kv.at[:, z],
                send_sem=z_send.at[step - 1],
                recv_sem=z_recv.at[step - 1],
                device_id={"mp": near(0, step)},
                device_id_type=MESH,
            )
        )
        z_copies[-1].start()
    all_kv[:, z] = column_kv[:, z // 4]

    lane = lax.broadcasted_iota(jnp.int32, (QB, HD), 1)
    even = lax.rem(lane, 2) == 0
    for t in range(3):
        rows = pl.ds(t * QB, QB)
        scale = scale_of(rows)
        for h in range(2):
            query = acc[rows, h * HD : (h + 1) * HD] * scale
            swapped = jnp.where(even, pltpu.roll(query, HD - 1, 1), pltpu.roll(query, 1, 1))
            rotated = query * cos_q[rows] + swapped * sin_q[rows]
            q_rot[rows, h * HD : (h + 1) * HD] = rotated.astype(BF16)

    for key in KEYS:
        passed(key).wait_send()
    for shift in shifts:
        shift.wait_send()
    for copy in x_copies:
        copy.wait_send()
    for copy in z_copies:
        copy.wait()

    want = lax.broadcasted_iota(jnp.int32, (512, 512), 0)
    have = lax.broadcasted_iota(jnp.int32, (512, 512), 1)
    channel = lax.rem(want, 128)
    source = 16 * (channel // 4) + 4 * (want // 128) + lax.rem(channel, 4)
    pick = (have == source).astype(F32).astype(BF16)
    for t in range(3):
        arrived = all_kv[:, :, t].reshape(512, 128)
        sorted_rows = jnp.dot(pick, arrived, preferred_element_type=F32).astype(BF16)
        for half in range(2):
            columns = slice(t * QB + half * 128, t * QB + half * 128 + 128)
            keys[:, columns] = sorted_rows[256 * half : 256 * half + 128]
            values[:, columns] = sorted_rows[256 * half + 128 : 256 * half + 256]

    for t in range(3):
        rows = slice(t * QB, (t + 1) * QB)
        reach = (t + 1) * QB
        token = lax.broadcasted_iota(jnp.int32, (QB, reach), 0) + t * QB
        causal = token >= lax.broadcasted_iota(jnp.int32, (QB, reach), 1)
        for h in range(2):
            scores = jnp.dot(
                q_rot[rows, h * HD : (h + 1) * HD], keys[:, :reach], preferred_element_type=F32
            ) * (1.0 / math.sqrt(HD))
            scores = jnp.where(causal, scores, -1e30)
            exponent = jnp.exp(scores - jnp.max(scores, axis=1, keepdims=True))
            probs = (exponent / jnp.sum(exponent, axis=1, keepdims=True)).astype(BF16)
            mixed = lax.dot_general(
                probs, values[:, :reach], (((1,), (1,)), ((), ())), preferred_element_type=F32
            )
            context[rows, h * HD : (h + 1) * HD] = mixed.astype(BF16)

    def project_out(unit, carry):
        columns = pl.ds(pl.multiple_of(unit * 256, 256), 256)
        rows = pl.ds(pl.multiple_of(unit * UNIT, UNIT), UNIT)
        product = jnp.dot(context[...], wo[:, columns], preferred_element_type=F32)
        for owner in range(N):
            mine = product[owner * ROWS : (owner + 1) * ROWS]
            term[owner, rows] = jnp.concatenate([mine[:, :128], mine[:, 128:]], axis=0).astype(BF16)
        return carry

    def handed(key):
        _, (low, high), at = SCATTER[key]
        size = (high - low) * UNIT
        return pltpu.make_async_remote_copy(
            src_ref=term.at[near(*seen_from_receiver(key, at)), pl.ds(low * UNIT, size)],
            dst_ref=landed.at[pl.ds(SLOT[key], size)],
            send_sem=scatter_send.at[NUMBER[key]],
            recv_sem=scatter_recv.at[NUMBER[key]],
            device_id={"mp": near(*STEP[OPPOSITE[key[0]]])},
            device_id_type=MESH,
        )

    here = set()

    def landing(key):
        if key not in here:
            here.add(key)
            handed(key).wait_recv()

    loads[3].wait()
    done = set()
    start, _ = in_order(SCATTER, 2 * 128 * UNIT)
    for key in sorted(start, key=start.get):
        before, (low, high), at = SCATTER[key]
        missing = [u for u in range(low, high) if u not in done]
        if missing:
            done.update(missing)
            lax.fori_loop(missing[0], missing[-1] + 1, project_out, 0)
        for other in before:
            landing(other)
        if before:
            owner = near(*seen_from_receiver(key, at))
            edges = {low, high}
            for other in before:
                edges.update(e for e in SCATTER[other][1] if low < e < high)
            edges = sorted(edges)
            for a, b in zip(edges, edges[1:]):
                rows = pl.ds(a * UNIT, (b - a) * UNIT)
                total = term[owner, rows].astype(F32)
                for other in before:
                    l, h = SCATTER[other][1]
                    if l <= a and b <= h:
                        total += landed[pl.ds(SLOT[other] + (a - l) * UNIT, (b - a) * UNIT)].astype(F32)
                term[owner, rows] = total.astype(BF16)
        handed(key).start()

    first = me * ROWS
    offset = lax.rem(me, 2) * 8
    window = pl.ds(pl.multiple_of(first - offset, 16), ROWS + 8)
    last = [key for key in KEYS if not GATHER[key][0]]
    for unit in range(D // 256):
        total = term[me, unit * UNIT : (unit + 1) * UNIT].astype(F32)
        for key in last:
            low, high = SCATTER[key][1]
            if low <= unit < high:
                landing(key)
                at = SLOT[key] + (unit - low) * UNIT
                total += landed[at : at + UNIT].astype(F32)
        total = jnp.concatenate([total[:ROWS], total[ROWS:]], axis=1)
        wide = hidden[unit, window].astype(F32)
        residual = jnp.where(offset == 0, wide[:ROWS], wide[8:])
        columns = slice(unit * WIDTH, (unit + 1) * WIDTH)
        attended[0, :, columns] = total.astype(BF16)
        stream[0, :, columns] = (residual + total).astype(BF16)
    for key in KEYS:
        handed(key).wait_send()


def layer(arriving, norm_gain, w_query, w_key, w_value, w_out):
    any_space = pl.BlockSpec(memory_space=pl.ANY)
    vmem = pl.BlockSpec(memory_space=pltpu.VMEM)
    out = jax.ShapeDtypeStruct((1, ROWS, D), BF16)
    dma = pltpu.SemaphoreType.DMA
    return pl.pallas_call(
        kernel,
        out_shape=(out, out),
        in_specs=[vmem, vmem, any_space, any_space, any_space, any_space],
        out_specs=(vmem, vmem),
        scratch_shapes=[
            pltpu.VMEM((N, LENGTH, WIDTH), BF16),
            pltpu.VMEM((WIDTH, D), BF16),
            pltpu.VMEM((2, 32, D), BF16),
            pltpu.VMEM((128, D), BF16),
            pltpu.VMEM((WIDTH, D), BF16),
            pltpu.VMEM((LENGTH, WIDTH + 128), F32),
            pltpu.VMEM((LENGTH, 128), F32),
            pltpu.VMEM((LENGTH, HD), F32),
            pltpu.VMEM((LENGTH, HD), F32),
            pltpu.VMEM((LENGTH, HD), F32),
            pltpu.VMEM((LENGTH, WIDTH), BF16),
            pltpu.VMEM((KV_HEADS, 3, 16, 128), BF16),
            pltpu.VMEM((X, 2, 3, 16, 128), BF16),
            pltpu.VMEM((X, Z, 3, 16, 128), BF16),
            pltpu.VMEM((HD, LENGTH), BF16),
            pltpu.VMEM((HD, LENGTH), BF16),
            pltpu.VMEM((LENGTH, WIDTH), BF16),
            pltpu.VMEM((N, D // 128 * ROWS, 128), BF16),
            pltpu.VMEM((LANDED, 128), BF16),
            dma((4,)),
            dma((2,)),
            dma((2,)),
            dma((len(KEYS),)),
            dma((len(KEYS),)),
            dma((X - 1,)),
            dma((X - 1,)),
            dma((Z - 1,)),
            dma((Z - 1,)),
            dma((len(KEYS),)),
            dma((len(KEYS),)),
        ],
        compiler_params=pltpu.CompilerParams(
            collective_id=0, has_side_effects=True, vmem_limit_bytes=67043328
        ),
    )(arriving, norm_gain, w_query, w_key, w_value, w_out)


def solution(mesh):
    return jax.shard_map(
        layer,
        mesh=mesh,
        in_specs=(
            P("section", None, "mp"),
            P("section", None),
            P("section", "mp", None),
            P("section", "mp", None),
            P("section", "mp", None),
            P("section", "mp", None),
        ),
        out_specs=(P("section", "mp", None), P("section", "mp", None)),
        check_vma=False,
    )
```

time: 278 us -> 175 us (0.63)
  Pallas kernels: 267 us -> 171 us
  other arithmetic: 4.19 us -> 0 us
    pallas_call x1, Pallas kernels: 267 us -> 171 us  [layer(): pl.pallas_call(kernel, out_shape=(out, out), in_specs=[vmem, vmem, any_sp...]
    select_n x2 -> x0, other arithmetic: 4.17 us -> none  [the longest x1 4.16 us: tables(): jnp.where(lanes[None, :] < 64, jnp.where(key_lane, jnp.cos(turn), 1.0), j...]
where the time goes in v2:
time: 175 us
  Pallas kernels  171 us (98%)
  local copies, waits for them, and re-layouts  3.53 us (2%)
    pallas_call x1, Pallas kernels, layer(): pl.pallas_call(kernel, out_shape=(out, out), in_specs=[vmem, vmem, any_sp...  171 us
    unnamed x2, local copies, waits for them, and re-layouts  3.53 us

profile of v2, /device:TPU:8, one launch (start us, length us, event | category | flops | bytes accessed | tf_op | source)
XLA Modules:
  0.0 174.8 jit_solution(18001477699350374861)
XLA Ops:
  0.6 170.6 %shard_map.77 = (bf16[1,24,8192]{2,1,0:T(8,128)(2,1)}, bf16[1,24,8192]{2,1,0:T(8,128)(2,1)}) custom-call(bf16[1,768,256]{2,1,0:T(8,128)(2,1)} %arriving.1, bf16[1,8192]{1,0:T(2,128)(2,1)} %gain.1, bf16[1,256,8192]{2,1,0:T(8,128)(2,1)} %w_query.1, bf16[1,32,8192]{2,1,0:T(8,128)(2,1)} %w_key.1, bf16[1,32,8192]{2,1,0:T(8,128)(2,1)} %w_value.1, ...), custom_call_target="tpu_custom_call" | custom-call | tf_op jit(solution)/shard_map/pallas_call | solution.py:466
  171.3 1.8 %copy.10 = bf16[1,24,8192]{2,1,0:T(8,128)(2,1)} copy(bf16[1,24,8192]{2,1,0:T(8,128)(2,1)} %get-tuple-element.4) | data formatting | bytes 786432
  173.0 1.8 %copy.11 = bf16[1,24,8192]{2,1,0:T(8,128)(2,1)} copy(bf16[1,24,8192]{2,1,0:T(8,128)(2,1)} %get-tuple-element.5) | data formatting | bytes 786432

commit v3 on v2

v3 whole, which is shorter than its diff:
```python
import math

import jax
import jax.numpy as jnp
from jax import lax
from jax.experimental import pallas as pl
from jax.experimental.pallas import tpu as pltpu
from jax.sharding import PartitionSpec as P

MESH = pl.DeviceIdType.MESH
BF16 = jnp.bfloat16
F32 = jnp.float32

X = 4
Z = 8
N = X * Z
SECTIONS = 8
LENGTH = 768
D = 8192
HD = 128
KV_HEADS = 8
WIDTH = D // N
ROWS = LENGTH // N
QB = 256
SPAN = ROWS * Z
TILE = 256
TILES = D // X // TILE
GROUPS = TILES // 2
BAND = X * ROWS

ROPE_BASE = 500000.0
EPS = 1e-05

LINKS = ("x+", "x-", "z+", "z-")
STEP = {"x+": (1, 0), "x-": (-1, 0), "z+": (0, 1), "z-": (0, -1)}
GATHER_CUTS = (0, 192, 384, 576, 768)
FAR_TILES = {"x+": (0, 1, 4, 5), "x-": (2, 3, 6, 7)}
NEAREST_LAST = (4, 3, -3, 2, -2, 1, -1, 0)


def plan(cuts):
    copies = {}
    n = 0
    a0, a1, a2, b1, b2 = cuts
    for sign in (1, -1):
        x_link, z_link = ("x+", "z+") if sign == 1 else ("x-", "z-")
        half_a = (a0, a1) if sign == 1 else (a1, a2)
        half_b = (a2, b1) if sign == 1 else (b1, b2)
        copies[x_link, n, "A", 0] = ((), (a0, a2), (0, 0))
        copies[x_link, n, "A", 1] = (((x_link, n, "A", 0),), half_a, (-sign, 0))
        for o in (0, -1, 1, -2, 2, -3, 3, 4):
            if o == 0:
                wanted = ()
            elif o == 4:
                wanted = (("z+", n, "B", 3), ("z-", n, "B", 3))
            else:
                wanted = (("z+" if o < 0 else "z-", n, "B", abs(o) - 1),)
            copies[x_link, n, "B", o] = (wanted, (a2, b2), (0, o))
            copies[x_link, n, "C", o] = (((x_link, n, "B", o),), half_b, (-sign, o))
        for hop in range(4):
            wanted = ((z_link, n, "B", hop - 1),) if hop else ()
            copies[z_link, n, "B", hop] = (wanted, half_b if hop == 3 else (a2, b2), (0, -sign * hop))
        for i in (0, -1, 1, 2):
            ends = (("x+", n, "A", 1), ("x-", n, "A", 1))
            first = {0: (), -1: (("x+", n, "A", 0),), 1: (("x-", n, "A", 0),), 2: ends}[i]
            for hop in range(4):
                wanted = ((z_link, n, "A", hop - 1, i),) if hop else first
                copies[z_link, n, "A", hop, i] = (wanted, half_a if hop == 3 else (a0, a2), (i, -sign * hop))
    return copies


def in_order(copies, ready_at, rate=46.6e3, latency=2.5, queue=2):
    length = {key: size / rate for key, (_, size) in copies.items()}
    after = {key: [] for key in copies}
    for key, (wanted, _) in copies.items():
        for other in wanted:
            after[other].append(key)
    chain = {}

    def chain_of(key):
        if key not in chain:
            chain[key] = length[key] + max([chain_of(k) for k in after[key]], default=0.0)
        return chain[key]

    left, ready, queued = list(copies), {link: [] for link in LINKS}, {link: [] for link in LINKS}
    free = {link: 0.0 for link in LINKS}
    arrival, start, now = {}, {}, 0.0
    while left or any(ready.values()):
        for key in list(left):
            if ready_at(key) <= now + 1e-9 and all(k in arrival and arrival[k] <= now + 1e-9 for k in copies[key][0]):
                left.remove(key)
                ready[key[0]].append(key)
        for link in LINKS:
            queued[link] = [t for t in queued[link] if t > now + 1e-9]
            while ready[link] and len(queued[link]) < queue:
                key = max(ready[link], key=lambda k: (-k[1], chain_of(k)))
                ready[link].remove(key)
                start[key] = now
                free[link] = max(now, free[link]) + length[key]
                queued[link].append(free[link])
                arrival[key] = free[link] + latency
        times = [t for t in arrival.values() if t > now + 1e-9] + [t for q in queued.values() for t in q if t > now + 1e-9]
        times += [ready_at(key) for key in left if ready_at(key) > now + 1e-9]
        now = min(times, default=now)
    return start, arrival


def seen_from_receiver(key, at):
    dx, dz = STEP[key[0]]
    return (at[0] - dx) % X, (at[1] - dz) % Z


GATHER = plan(GATHER_CUTS)
KEYS = list(GATHER)
NUMBER = {key: n for n, key in enumerate(KEYS)}


def kernel(
    arriving, gain, w_query, w_key, w_value, w_out,
    sums, entering,
    hidden, wq, wkv_raw, wkv, wo, stage, acc, squares, cos_q, sin_q, turn_kv, q_rot, own_kv, column_kv, all_kv, keys, values,
    own_context, context, term, landed, leaving, final,
    w_sem, wo_sem, shift_send, shift_recv, gather_send, gather_recv, weight_send, weight_recv, x_send, x_recv, z_send, z_recv,
    context_send, context_recv, scatter_send, scatter_recv, final_send, final_recv,
):
    me = lax.axis_index("mp")
    section = lax.axis_index("section")
    x, z = me // Z, lax.rem(me, Z)

    def near(dx, dz):
        return lax.rem(x + dx % X, X) * Z + lax.rem(z + dz % Z, Z)

    loads = [
        pltpu.make_async_copy(w_key.at[0], wkv_raw.at[0], w_sem.at[0]),
        pltpu.make_async_copy(w_value.at[0], wkv_raw.at[1], w_sem.at[1]),
        pltpu.make_async_copy(w_query.at[0], wq, w_sem.at[2]),
    ]

    def out_weights(place, tile):
        return w_out.at[0, :, pl.ds(pl.multiple_of(place * (D // X) + tile * TILE, TILE), TILE)]

    def from_place(place):
        return pl.ds(pl.multiple_of(place * WIDTH, WIDTH), WIDTH)

    for tile in range(TILES):
        loads.append(pltpu.make_async_copy(out_weights(x, tile), wo.at[tile, from_place(x)], wo_sem.at[tile]))
    for load in loads:
        load.start()

    barrier = pltpu.get_barrier_semaphore()
    for step in range(1, X):
        pl.semaphore_signal(barrier, inc=1, device_id={"mp": near(step, 0)}, device_id_type=MESH)
    for step in range(1, Z):
        pl.semaphore_signal(barrier, inc=1, device_id={"mp": near(0, step)}, device_id_type=MESH)
    for step in (1, SECTIONS - 1):
        pl.semaphore_signal(
            barrier, inc=1, device_id={"section": lax.rem(section + step, SECTIONS)}, device_id_type=MESH
        )
    pl.semaphore_wait(barrier, (X - 1) + (Z - 1) + 2)

    parts = (GATHER_CUTS[0:3:2], GATHER_CUTS[2:5:2])
    shifts = []
    for s, (low, high) in enumerate(parts):
        rows = pl.ds(low, high - low)
        shifts.append(
            pltpu.make_async_remote_copy(
                src_ref=arriving.at[0, rows],
                dst_ref=hidden.at[me, rows],
                send_sem=shift_send.at[s],
                recv_sem=shift_recv.at[s],
                device_id={"section": lax.rem(section + 1, SECTIONS)},
                device_id_type=MESH,
            )
        )
        shifts[-1].start()

    loads[0].wait()
    loads[1].wait()
    out_row = lax.broadcasted_iota(jnp.int32, (128, 64), 0)
    raw_row = lax.broadcasted_iota(jnp.int32, (128, 64), 1)
    head, j = lax.rem(out_row, 64) // 8, lax.rem(out_row, 8)
    channel = lax.rem(j, 4)
    turned = jnp.where(out_row >= 64, channel + 1 - 2 * lax.rem(channel, 2), channel)
    source = (j // 4) * 32 + (turned // 2) * 16 + head * 2 + lax.rem(turned, 2)
    pick = (raw_row == source).astype(F32).astype(BF16)
    for part in range(8):
        columns = pl.ds(part * (D // 8), D // 8)
        raw = jnp.concatenate([wkv_raw[0, :, columns], wkv_raw[1, :, columns]], axis=0)
        wkv[:, columns] = jnp.dot(pick, raw, preferred_element_type=F32).astype(BF16)

    def passed(key):
        _, (low, high), at = GATHER[key]
        block = hidden.at[near(*at), pl.ds(low, high - low)]
        return pltpu.make_async_remote_copy(
            src_ref=block,
            dst_ref=block,
            send_sem=gather_send.at[NUMBER[key]],
            recv_sem=gather_recv.at[NUMBER[key]],
            device_id={"mp": near(*STEP[key[0]])},
            device_id_type=MESH,
        )

    def weights(key):
        link, _, kind, i = key
        way = STEP[link][0]
        side = 0 if way == 1 else 1
        slot = {"W": 0, "V": TILES, "U": TILES + TILES // 2}[kind] + i
        if kind == "W":
            source, target = out_weights(lax.rem(x + way + X, X), i), wo.at[i, from_place(x)]
        elif kind == "V":
            source, target = out_weights(lax.rem(x + 2, X), FAR_TILES[link][i]), stage.at[side, i]
        else:
            source, target = stage.at[side, i], wo.at[FAR_TILES[link][i], from_place(lax.rem(x - way + X, X))]
        return pltpu.make_async_remote_copy(
            src_ref=source,
            dst_ref=target,
            send_sem=weight_send.at[side, slot],
            recv_sem=weight_recv.at[side, slot],
            device_id={"mp": near(way, 0)},
            device_id_type=MESH,
        )

    def arrived_block(key):
        _, (low, high), at = GATHER[key]
        block = hidden.at[near(*seen_from_receiver(key, at)), pl.ds(low, high - low)]
        return pltpu.make_async_remote_copy(
            src_ref=block,
            dst_ref=block,
            send_sem=gather_send.at[NUMBER[key]],
            recv_sem=gather_recv.at[NUMBER[key]],
            device_id={"mp": near(*STEP[key[0]])},
            device_id_type=MESH,
        )

    started_rows = set()

    def project(part, at):
        owner = near(*at)
        rows = pl.ds(parts[part][0], parts[part][1] - parts[part][0])
        columns = pl.ds(pl.multiple_of(owner * WIDTH, WIDTH), WIDTH)
        block = hidden[owner, rows].astype(F32)
        squared = block * block
        squared = squared[:, :128] + squared[:, 128:]
        scaled = (block * gain[:, columns].astype(F32)).astype(BF16)
        contract = (((1,), (1,)), ((), ()))
        queries = lax.dot_general(scaled, wq[:, columns], contract, preferred_element_type=F32)
        others = lax.dot_general(scaled, wkv[:, columns], contract, preferred_element_type=F32)
        if part not in started_rows:
            started_rows.add(part)
            squares[rows] = squared
            acc[rows, :WIDTH] = queries
            acc[rows, WIDTH:] = others
        else:
            squares[rows] += squared
            acc[rows, :WIDTH] += queries
            acc[rows, WIDTH:] += others

    def rotary_table(i):
        size = 64
        rows = pl.ds(i * size, size)
        lane = lax.broadcasted_iota(jnp.int32, (size, HD), 1)
        token = (lax.broadcasted_iota(jnp.int32, (size, HD), 0) + i * size).astype(F32)
        sign = jnp.where(lax.rem(lane, 2) == 0, -1.0, 1.0)

        def angle(pair):
            return token * jnp.exp(pair.astype(F32) * (-2.0 * math.log(ROPE_BASE) / HD))

        turn = angle(lane // 2)
        cos_q[rows] = jnp.cos(turn)
        sin_q[rows] = jnp.sin(turn) * sign
        j = lax.rem(lane, 8)
        turn = angle(2 * me + lax.rem(j, 4) // 2)
        stay = jnp.where(j < 4, jnp.cos(turn), 1.0)
        cross = jnp.where(j < 4, jnp.sin(turn) * sign, 0.0)
        turn_kv[rows] = jnp.where(lane < 64, stay, cross)

    def scale_of(rows):
        mean = jnp.sum(squares[rows], axis=1, keepdims=True) * (1.0 / D)
        return lax.rsqrt(mean + EPS)

    blocks = ((0, 1, 2),)
    x_copies, z_copies = {}, {}

    def send_along_x(n):
        for t in blocks[n]:
            rows = pl.ds(t * QB, QB)
            both = acc[rows, WIDTH:] * scale_of(rows) * turn_kv[rows]
            ready = (both + pltpu.roll(both, 64, 1)).T
            for h in range(KV_HEADS):
                tile = ready[8 * h : 8 * h + 8]
                own_kv[h, t] = jnp.concatenate([tile[:, :128], tile[:, 128:]], axis=0).astype(BF16)
        these = pl.ds(blocks[n][0], len(blocks[n]))
        for step in range(1, X):
            to = lax.rem(x + step, X)
            copy = pltpu.make_async_remote_copy(
                src_ref=own_kv.at[pl.ds(2 * to, 2), these],
                dst_ref=column_kv.at[x, :, these],
                send_sem=x_send.at[n, step - 1],
                recv_sem=x_recv.at[n, step - 1],
                device_id={"mp": near(step, 0)},
                device_id_type=MESH,
            )
            copy.start()
            x_copies[n, step] = copy
        for h in range(2):
            column_kv[x, h, these] = own_kv[2 * x + h, these]

    def send_along_z(n):
        these = pl.ds(blocks[n][0], len(blocks[n]))
        for step in range(1, X):
            x_copies[n, step].wait_recv()
        for step in range(1, Z):
            to = lax.rem(z + step, Z)
            copy = pltpu.make_async_remote_copy(
                src_ref=column_kv.at[:, to // 4, these],
                dst_ref=all_kv.at[:, z, these],
                send_sem=z_send.at[n, step - 1],
                recv_sem=z_recv.at[n, step - 1],
                device_id={"mp": near(0, step)},
                device_id_type=MESH,
            )
            copy.start()
            z_copies[n, step] = copy
        for t in blocks[n]:
            all_kv[:, z, t] = column_kv[:, z // 4, t]

    def turn_queries(t):
        lane = lax.broadcasted_iota(jnp.int32, (QB, HD), 1)
        even = lax.rem(lane, 2) == 0
        rows = pl.ds(t * QB, QB)
        scale = scale_of(rows)
        for h in range(2):
            query = acc[rows, h * HD : (h + 1) * HD] * scale
            swapped = jnp.where(even, pltpu.roll(query, HD - 1, 1), pltpu.roll(query, 1, 1))
            rotated = query * cos_q[rows] + swapped * sin_q[rows]
            q_rot[rows, h * HD : (h + 1) * HD] = rotated.astype(BF16)

    def sort_keys(n):
        for step in range(1, Z):
            z_copies[n, step].wait_recv()
        want = lax.broadcasted_iota(jnp.int32, (512, 512), 0)
        have = lax.broadcasted_iota(jnp.int32, (512, 512), 1)
        channel = lax.rem(want, 128)
        source = 16 * (channel // 4) + 4 * (want // 128) + lax.rem(channel, 4)
        pick = (have == source).astype(F32).astype(BF16)
        for t in blocks[n]:
            arrived = all_kv[:, :, t].reshape(512, 128)
            sorted_rows = jnp.dot(pick, arrived, preferred_element_type=F32).astype(BF16)
            for half in range(2):
                columns = slice(t * QB + half * 128, t * QB + half * 128 + 128)
                keys[:, columns] = sorted_rows[256 * half : 256 * half + 128]
                values[:, columns] = sorted_rows[256 * half + 128 : 256 * half + 256]

    def attend(t, h):
        rows = slice(t * SPAN, (t + 1) * SPAN)
        reach = -(-(t + 1) * SPAN // 128) * 128
        token = lax.broadcasted_iota(jnp.int32, (SPAN, reach), 0) + t * SPAN
        causal = token >= lax.broadcasted_iota(jnp.int32, (SPAN, reach), 1)
        scores = jnp.dot(
            q_rot[rows, h * HD : (h + 1) * HD], keys[:, :reach], preferred_element_type=F32
        ) * (1.0 / math.sqrt(HD))
        scores = jnp.where(causal, scores, -1e30)
        exponent = jnp.exp(scores - jnp.max(scores, axis=1, keepdims=True))
        probs = (exponent / jnp.sum(exponent, axis=1, keepdims=True)).astype(BF16)
        mixed = lax.dot_general(
            probs, values[:, :reach], (((1,), (1,)), ((), ())), preferred_element_type=F32
        )
        for place in range(Z):
            own_context[place, t * ROWS : (t + 1) * ROWS, h * HD : (h + 1) * HD] = mixed[place * ROWS : (place + 1) * ROWS]

    own_part = {("A", 0): 0, ("B", 0): 1, ("A", 0, 0): 0}
    own_at = (4.5, 7.0)
    copies = {key: (wanted, (rows[1] - rows[0]) * 2 * WIDTH) for key, (wanted, rows, _) in GATHER.items()}
    for link in ("x+", "x-"):
        for i in range(TILES // 2):
            copies[link, 1, "V", i] = ((), WIDTH * TILE * 2)
            copies[link, 1, "U", i] = (((link, 1, "V", i),), WIDTH * TILE * 2)

    def own_ready(key):
        return 0.0 if key[1] or GATHER[key][0] else own_at[own_part[key[2:]]]

    start, arrival = in_order(copies, own_ready)
    bringing = {((0, 0), part): [] for part in range(len(parts))}
    for key, (_, (low, _), at) in GATHER.items():
        part = int(low >= parts[1][0])
        bringing.setdefault((seen_from_receiver(key, at), part), []).append(key)
    events = [(t, 0, "weights" if key[1] else "pass", key) for key, t in start.items()]
    events += [
        (max([arrival[k] + 1.0 for k in by], default=own_at[which[1]] + 0.1), 1, "project", which)
        for which, by in bringing.items()
    ]
    events += [(5.0 + 1.5 * i, 2, "table", i) for i in range(12)]
    events.sort(key=lambda event: event[:2])
    waited = set()

    def need(key):
        if key not in waited:
            waited.add(key)
            (weights if key[1] else arrived_block)(key).wait_recv()

    def need_own(part):
        if ("own", part) not in waited:
            waited.add(("own", part))
            shifts[part].wait_recv()

    query_weights_here = False
    for _, _, what, which in events:
        if what == "pass":
            for key in GATHER[which][0]:
                need(key)
            if not GATHER[which][0]:
                need_own(own_part[which[2:]])
            passed(which).start()
        elif what == "project":
            if not query_weights_here:
                query_weights_here = True
                loads[2].wait()
            for key in bringing[which]:
                need(key)
            if not bringing[which]:
                need_own(which[1])
            project(which[1], which[0])
        elif what == "weights":
            for key in copies[which][0]:
                need(key)
            weights(which).start()
        else:
            rotary_table(which)

    send_along_x(0)
    for t in range(3):
        turn_queries(t)
    send_along_z(0)
    for i in range(TILES // 2):
        for link in ("x+", "x-"):
            weights((link, 1, "W", i)).start()
    for key in KEYS:
        passed(key).wait_send()
    for shift in shifts:
        shift.wait_send()
    first = me * ROWS
    offset = lax.rem(me, 2) * 8
    window = pl.ds(pl.multiple_of(first - offset, 16), ROWS + 8)
    for unit in range(N):
        wide = hidden[unit, window].astype(F32)
        residual = jnp.where(offset == 0, wide[:ROWS], wide[8:])
        entering[0, :, unit * WIDTH : (unit + 1) * WIDTH] = residual.astype(BF16)
    sort_keys(0)
    for t in range(X):
        for h in range(2):
            attend(t, h)
    for place in range(Z):
        context[x, place] = own_context[place].astype(BF16)
    for copy in list(x_copies.values()) + list(z_copies.values()):
        copy.wait_send()

    def hand_context(link, hop, i):
        way = STEP[link][0]
        side = 0 if way == 1 else 1
        place = lax.rem(z + NEAREST_LAST[i] + Z, Z)
        if hop == 0:
            part = context.at[x, place]
        else:
            part = context.at[lax.rem(x - way + X, X), place, pl.ds(side * (BAND // 2), BAND // 2)]
        return pltpu.make_async_remote_copy(
            src_ref=part,
            dst_ref=part,
            send_sem=context_send.at[side, hop, i],
            recv_sem=context_recv.at[side, hop, i],
            device_id={"mp": near(way, 0)},
            device_id_type=MESH,
        )

    def make_terms(i, half):
        place = lax.rem(z + NEAREST_LAST[i] + Z, Z)
        mixed = jnp.concatenate([context[c, place] for c in range(X)], axis=1)
        for tile in range(half * GROUPS, (half + 1) * GROUPS):
            product = jnp.dot(mixed, wo[tile], preferred_element_type=F32)
            columns = slice(tile % 2 * TILE, (tile % 2 + 1) * TILE)
            term[i, tile // 2, :, columns] = product.astype(BF16)

    def handed(way, step, group):
        side = 0 if way == 1 else 1
        return pltpu.make_async_remote_copy(
            src_ref=term.at[NEAREST_LAST.index(way * (4 - step) if step else 4), group],
            dst_ref=landed.at[side, step, group],
            send_sem=scatter_send.at[side, step, group],
            recv_sem=scatter_recv.at[side, step, group],
            device_id={"mp": near(0, way)},
            device_id_type=MESH,
        )

    def starts_here(way, step, group):
        return step == 0 or (step == 1 and group % 2 != (0 if way == 1 else 1))

    def hand_on(way, step, group):
        if not starts_here(way, step, group):
            handed(way, step - 1, group).wait_recv()
            i = NEAREST_LAST.index(way * (4 - step))
            total = term[i, group].astype(F32) + landed[0 if way == 1 else 1, step - 1, group].astype(F32)
            term[i, group] = total.astype(BF16)
        handed(way, step, group).start()

    def ready_ones(i, half):
        groups = (2 * half, 2 * half + 1)
        away = NEAREST_LAST[i]
        if away == 4:
            every = [(1, 0, groups[0]), (-1, 0, groups[1])]
        elif away == 0:
            every = []
        else:
            way = 1 if away > 0 else -1
            every = [(way, 4 - abs(away), g) for g in groups]
        now = [c for c in every if starts_here(*c)]
        later = [c for c in every if not starts_here(*c)]
        return now, sorted(later, key=lambda c: (c[2] % 2 == (0 if c[0] == 1 else 1)) if c[1] > 1 else 0)

    def leave(group, step):
        to = lax.rem(x + step, X)
        return pltpu.make_async_remote_copy(
            src_ref=leaving.at[to, group],
            dst_ref=final.at[x, group],
            send_sem=final_send.at[step - 1, group],
            recv_sem=final_recv.at[step - 1, group],
            device_id={"mp": near(step, 0)},
            device_id_type=MESH,
        )

    def finish(group):
        total = term[NEAREST_LAST.index(0), group].astype(F32)
        for way in (1, -1):
            handed(way, 3, group).wait_recv()
            total += landed[0 if way == 1 else 1, 3, group].astype(F32)
        for to in range(X):
            mine = total[to * ROWS : (to + 1) * ROWS]
            leaving[to, group] = jnp.concatenate([mine[:, :TILE], mine[:, TILE:]], axis=0).astype(BF16)
        for step in range(1, X):
            leave(group, step).start()
        final[x, group] = leaving[x, group]

    def write(group):
        for step in range(1, X):
            leave(group, step).wait_recv()
        for place in range(X):
            total = final[place, group].astype(F32)
            at = place * (D // X) + group * 2 * TILE
            sums[0, :, at : at + TILE] = total[:ROWS]
            sums[0, :, at + TILE : at + 2 * TILE] = total[ROWS:]

    def weights_of(half):
        for tile in range(half * GROUPS, (half + 1) * GROUPS):
            loads[3 + tile].wait()
            for link in ("x+", "x-"):
                need((link, 1, "W", tile))
                if tile in FAR_TILES[link]:
                    need((link, 1, "U", FAR_TILES[link].index(tile)))

    def pass_context(j):
        for link in ("x+", "x-"):
            hand_context(link, 0, j).wait_recv()
        for link in ("x+", "x-"):
            hand_context(link, 1, j).start()
            if j + 4 < Z:
                hand_context(link, 0, j + 4).start()

    for j in range(4):
        for link in ("x+", "x-"):
            hand_context(link, 0, j).start()
    pass_context(0)
    pass_context(1)
    weights_of(0)
    lagging = []
    for i in range(Z):
        for j in (2 * i + 2, 2 * i + 3):
            if j < Z:
                pass_context(j)
        if 2 * i + 3 == Z - 1:
            for tile in range(TILES // 2, TILES):
                for link in ("x+", "x-"):
                    weights((link, 1, "W", tile)).start()
        for link in ("x+", "x-"):
            hand_context(link, 1, i).wait_recv()
        make_terms(i, 0)
        now, later = ready_ones(i, 0)
        for copy in now + lagging:
            hand_on(*copy)
        lagging = later
    weights_of(1)
    for i in range(Z):
        make_terms(i, 1)
        now, later = ready_ones(i, 1)
        for copy in now + lagging:
            hand_on(*copy)
        lagging = later
        if i == 3:
            finish(1)
            finish(0)
        if i == 6:
            write(1)
            write(0)
    for copy in lagging:
        hand_on(*copy)
    finish(3)
    finish(2)

    write(3)
    write(2)
    for link in ("x+", "x-"):
        for i in range(TILES):
            weights((link, 1, "W", i)).wait_send()
        for i in range(TILES // 2):
            weights((link, 1, "V", i)).wait_send()
            weights((link, 1, "U", i)).wait_send()
        for i in range(Z):
            for hop in range(2):
                hand_context(link, hop, i).wait_send()
    for way in (1, -1):
        for group in range(GROUPS):
            for step in range(4):
                if step or group % 2 == (0 if way == 1 else 1):
                    handed(way, step, group).wait_send()
    for group in range(GROUPS):
        for step in range(1, X):
            leave(group, step).wait_send()


def layer(arriving, norm_gain, w_query, w_key, w_value, w_out):
    any_space = pl.BlockSpec(memory_space=pl.ANY)
    vmem = pl.BlockSpec(memory_space=pltpu.VMEM)
    sums = jax.ShapeDtypeStruct((1, ROWS, D), F32)
    entering = jax.ShapeDtypeStruct((1, ROWS, D), BF16)
    dma = pltpu.SemaphoreType.DMA
    summed, residual = pl.pallas_call(
        kernel,
        out_shape=(sums, entering),
        in_specs=[vmem, vmem, any_space, any_space, any_space, any_space],
        out_specs=(vmem, vmem),
        scratch_shapes=[
            pltpu.VMEM((N, LENGTH, WIDTH), BF16),
            pltpu.VMEM((WIDTH, D), BF16),
            pltpu.VMEM((2, 32, D), BF16),
            pltpu.VMEM((128, D), BF16),
            pltpu.VMEM((TILES, X * WIDTH, TILE), BF16),
            pltpu.VMEM((2, TILES // 2, WIDTH, TILE), BF16),
            pltpu.VMEM((LENGTH, WIDTH + 128), F32),
            pltpu.VMEM((LENGTH, 128), F32),
            pltpu.VMEM((LENGTH, HD), F32),
            pltpu.VMEM((LENGTH, HD), F32),
            pltpu.VMEM((LENGTH, HD), F32),
            pltpu.VMEM((LENGTH, WIDTH), BF16),
            pltpu.VMEM((KV_HEADS, 3, 16, 128), BF16),
            pltpu.VMEM((X, 2, 3, 16, 128), BF16),
            pltpu.VMEM((X, Z, 3, 16, 128), BF16),
            pltpu.VMEM((HD, LENGTH), BF16),
            pltpu.VMEM((HD, LENGTH), BF16),
            pltpu.VMEM((Z, BAND, WIDTH), F32),
            pltpu.VMEM((X, Z, BAND, WIDTH), BF16),
            pltpu.VMEM((Z, GROUPS, BAND, 2 * TILE), BF16),
            pltpu.VMEM((2, 4, GROUPS, BAND, 2 * TILE), BF16),
            pltpu.VMEM((X, GROUPS, 2 * ROWS, TILE), BF16),
            pltpu.VMEM((X, GROUPS, 2 * ROWS, TILE), BF16),
            dma((3,)),
            dma((TILES,)),
            dma((2,)),
            dma((2,)),
            dma((len(KEYS),)),
            dma((len(KEYS),)),
            dma((2, 2 * TILES)),
            dma((2, 2 * TILES)),
            dma((1, X - 1)),
            dma((1, X - 1)),
            dma((1, Z - 1)),
            dma((1, Z - 1)),
            dma((2, 2, Z)),
            dma((2, 2, Z)),
            dma((2, 4, GROUPS)),
            dma((2, 4, GROUPS)),
            dma((X - 1, GROUPS)),
            dma((X - 1, GROUPS)),
        ],
        compiler_params=pltpu.CompilerParams(
            collective_id=0, has_side_effects=True, vmem_limit_bytes=67043328
        ),
    )(arriving, norm_gain, w_query, w_key, w_value, w_out)
    return summed.astype(BF16), (residual.astype(F32) + summed).astype(BF16)


def solution(mesh):
    return jax.shard_map(
        layer,
        mesh=mesh,
        in_specs=(
            P("section", None, "mp"),
            P("section", None),
            P("section", "mp", None),
            P("section", "mp", None),
            P("section", "mp", None),
            P("section", "mp", None),
        ),
        out_specs=(P("section", "mp", None), P("section", "mp", None)),
        check_vma=False,
    )
```

time: 175 us -> 163 us (0.931)
  Pallas kernels: 171 us -> 160 us
  local copies, waits for them, and re-layouts: 3.53 us -> 0 us
  other arithmetic: 0 us -> 2.44 us
    pallas_call x1, Pallas kernels: 171 us -> 160 us  [layer(): pl.pallas_call(kernel, out_shape=(sums, entering), in_specs=[vmem, vmem,...]
    unnamed x2 -> x0, local copies, waits for them, and re-layouts: 3.53 us -> none
    convert_element_type x0 -> x1, other arithmetic: none -> 2.44 us  [layer(): return (summed.astype(BF16), (residual.astype(F32) + summed).astype(BF16))]
where the time goes in v3:
time: 163 us
  Pallas kernels  160 us (98%)
  other arithmetic  2.44 us (1%)
    pallas_call x1, Pallas kernels, layer(): pl.pallas_call(kernel, out_shape=(sums, entering), in_specs=[vmem, vmem,...  160 us

profile of v3, /device:TPU:8, one launch (start us, length us, event | category | flops | bytes accessed | tf_op | source)
XLA Modules:
  0.0 163.2 jit_solution(122446219995579246)
XLA Ops:
  0.6 160.1 %shard_map.77 = (f32[1,24,8192]{2,1,0:T(8,128)}, bf16[1,24,8192]{2,1,0:T(8,128)(2,1)}) custom-call(bf16[1,768,256]{2,1,0:T(8,128)(2,1)} %arriving.1, bf16[1,8192]{1,0:T(2,128)(2,1)} %gain.1, bf16[1,256,8192]{2,1,0:T(8,128)(2,1)} %w_query.1, bf16[1,32,8192]{2,1,0:T(8,128)(2,1)} %w_key.1, bf16[1,32,8192]{2,1,0:T(8,128)(2,1)} %w_value.1, ...), custom_call_target="tpu_custom_call" | custom-call | tf_op jit(solution)/shard_map/pallas_call | solution.py:633
  160.7 2.4 %add_convert_fusion = (bf16[1,24,8192]{2,1,0:T(8,128)(2,1)}, bf16[1,24,8192]{2,1,0:T(8,128)(2,1)}) fusion(f32[1,24,8192]{2,1,0:T(8,128)} %get-tuple-element.4, bf16[1,24,8192]{2,1,0:T(8,128)(2,1)} %get-tuple-element.5), kind=kLoop, calls=%fused_computation | loop fusion | flops 786432 | bytes 1966080 | tf_op jit(solution)/shard_map/convert_element_type | solution.py:685

commit v4 on v3

--- a/solution.py
+++ b/solution.py
@@ -25,7 +25,7 @@
 SPAN = ROWS * Z
 TILE = 256
 TILES = D // X // TILE
-GROUPS = TILES // 2
+PAIRS = TILES // 2
 BAND = X * ROWS
 
 ROPE_BASE = 500000.0
@@ -34,7 +34,8 @@
 LINKS = ("x+", "x-", "z+", "z-")
 STEP = {"x+": (1, 0), "x-": (-1, 0), "z+": (0, 1), "z-": (0, -1)}
 GATHER_CUTS = (0, 192, 384, 576, 768)
-FAR_TILES = {"x+": (0, 1, 4, 5), "x-": (2, 3, 6, 7)}
+FAR_TILES = {"x+": (0, 2, 4, 6), "x-": (1, 3, 5, 7)}
+EARLY_FAR = 4
 NEAREST_LAST = (4, 3, -3, 2, -2, 1, -1, 0)
 
 
@@ -119,7 +120,7 @@
     arriving, gain, w_query, w_key, w_value, w_out,
     sums, entering,
     hidden, wq, wkv_raw, wkv, wo, stage, acc, squares, cos_q, sin_q, turn_kv, q_rot, own_kv, column_kv, all_kv, keys, values,
-    own_context, context, term, landed, leaving, final,
+    own_context, context, term, landed, whole, leaving, final,
     w_sem, wo_sem, shift_send, shift_recv, gather_send, gather_recv, weight_send, weight_recv, x_send, x_recv, z_send, z_recv,
     context_send, context_recv, scatter_send, scatter_recv, final_send, final_recv,
 ):
@@ -278,7 +279,7 @@
         mean = jnp.sum(squares[rows], axis=1, keepdims=True) * (1.0 / D)
         return lax.rsqrt(mean + EPS)
 
-    blocks = ((0, 1, 2),)
+    blocks = ((0,), (1,), (2,))
     x_copies, z_copies = {}, {}
 
     def send_along_x(n):
@@ -372,7 +373,7 @@
     own_at = (4.5, 7.0)
     copies = {key: (wanted, (rows[1] - rows[0]) * 2 * WIDTH) for key, (wanted, rows, _) in GATHER.items()}
     for link in ("x+", "x-"):
-        for i in range(TILES // 2):
+        for i in range(EARLY_FAR):
             copies[link, 1, "V", i] = ((), WIDTH * TILE * 2)
             copies[link, 1, "U", i] = (((link, 1, "V", i),), WIDTH * TILE * 2)
 
@@ -427,13 +428,18 @@
         else:
             rotary_table(which)
 
-    send_along_x(0)
+    for t in range(3):
+        send_along_x(t)
     for t in range(3):
         turn_queries(t)
-    send_along_z(0)
+    for t in range(3):
+        send_along_z(t)
     for i in range(TILES // 2):
         for link in ("x+", "x-"):
             weights((link, 1, "W", i)).start()
+    for i in range(EARLY_FAR, TILES // 2):
+        for link in ("x+", "x-"):
+            weights((link, 1, "V", i)).start()
     for key in KEYS:
         passed(key).wait_send()
     for shift in shifts:
@@ -445,8 +451,9 @@
         wide = hidden[unit, window].astype(F32)
         residual = jnp.where(offset == 0, wide[:ROWS], wide[8:])
         entering[0, :, unit * WIDTH : (unit + 1) * WIDTH] = residual.astype(BF16)
-    sort_keys(0)
     for t in range(X):
+        if t < 3:
+            sort_keys(t)
         for h in range(2):
             attend(t, h)
     for place in range(Z):
@@ -471,140 +478,153 @@
             device_id_type=MESH,
         )
 
-    def make_terms(i, half):
-        place = lax.rem(z + NEAREST_LAST[i] + Z, Z)
-        mixed = jnp.concatenate([context[c, place] for c in range(X)], axis=1)
-        for tile in range(half * GROUPS, (half + 1) * GROUPS):
-            product = jnp.dot(mixed, wo[tile], preferred_element_type=F32)
-            columns = slice(tile % 2 * TILE, (tile % 2 + 1) * TILE)
-            term[i, tile // 2, :, columns] = product.astype(BF16)
-
-    def handed(way, step, group):
+    def place_of(i):
+        return lax.rem(z + NEAREST_LAST[i] + Z, Z)
+
+    made = set()
+
+    def make_terms(i, tile):
+        if (i, tile) in made:
+            return
+        these = [n for n, away in enumerate(NEAREST_LAST) if abs(away) == abs(NEAREST_LAST[i])]
+        made.update((n, tile) for n in these)
+        for n in these:
+            for link in ("x+", "x-"):
+                need_late((link, "Q", n))
+        if tile not in made:
+            made.add(tile)
+            loads[3 + tile].wait()
+            for link in ("x+", "x-"):
+                need_late((link, "W", tile))
+                if tile in FAR_TILES[link]:
+                    need_late((link, "U", FAR_TILES[link].index(tile)))
+        mixed = [jnp.concatenate([context[c, place_of(n)] for c in range(X)], axis=1) for n in these]
+        product = jnp.dot(jnp.concatenate(mixed, axis=0), wo[tile], preferred_element_type=F32).astype(BF16)
+        for m, n in enumerate(these):
+            term[n, tile] = product[m * BAND : (m + 1) * BAND]
+
+    def handed(way, step, tile):
         side = 0 if way == 1 else 1
         return pltpu.make_async_remote_copy(
-            src_ref=term.at[NEAREST_LAST.index(way * (4 - step) if step else 4), group],
-            dst_ref=landed.at[side, step, group],
-            send_sem=scatter_send.at[side, step, group],
-            recv_sem=scatter_recv.at[side, step, group],
+            src_ref=term.at[NEAREST_LAST.index(way * (4 - step) if step else 4), tile],
+            dst_ref=landed.at[side, step, tile],
+            send_sem=scatter_send.at[side, step, tile],
+            recv_sem=scatter_recv.at[side, step, tile],
             device_id={"mp": near(0, way)},
             device_id_type=MESH,
         )
 
-    def starts_here(way, step, group):
-        return step == 0 or (step == 1 and group % 2 != (0 if way == 1 else 1))
-
-    def hand_on(way, step, group):
-        if not starts_here(way, step, group):
-            handed(way, step - 1, group).wait_recv()
+    def starts_here(way, step, tile):
+        return step == 0 or (step == 1 and tile % 2 != (0 if way == 1 else 1))
+
+    def hand_on(way, step, tile):
+        if not starts_here(way, step, tile):
+            handed(way, step - 1, tile).wait_recv()
             i = NEAREST_LAST.index(way * (4 - step))
-            total = term[i, group].astype(F32) + landed[0 if way == 1 else 1, step - 1, group].astype(F32)
-            term[i, group] = total.astype(BF16)
-        handed(way, step, group).start()
-
-    def ready_ones(i, half):
-        groups = (2 * half, 2 * half + 1)
-        away = NEAREST_LAST[i]
-        if away == 4:
-            every = [(1, 0, groups[0]), (-1, 0, groups[1])]
-        elif away == 0:
-            every = []
-        else:
-            way = 1 if away > 0 else -1
-            every = [(way, 4 - abs(away), g) for g in groups]
-        now = [c for c in every if starts_here(*c)]
-        later = [c for c in every if not starts_here(*c)]
-        return now, sorted(later, key=lambda c: (c[2] % 2 == (0 if c[0] == 1 else 1)) if c[1] > 1 else 0)
-
-    def leave(group, step):
+            total = term[i, tile].astype(F32) + landed[0 if way == 1 else 1, step - 1, tile].astype(F32)
+            term[i, tile] = total.astype(BF16)
+        handed(way, step, tile).start()
+
+    def leave(pair, step):
         to = lax.rem(x + step, X)
         return pltpu.make_async_remote_copy(
-            src_ref=leaving.at[to, group],
-            dst_ref=final.at[x, group],
-            send_sem=final_send.at[step - 1, group],
-            recv_sem=final_recv.at[step - 1, group],
+            src_ref=leaving.at[to, pair],
+            dst_ref=final.at[x, pair],
+            send_sem=final_send.at[step - 1, pair],
+            recv_sem=final_recv.at[step - 1, pair],
             device_id={"mp": near(step, 0)},
             device_id_type=MESH,
         )
 
-    def finish(group):
-        total = term[NEAREST_LAST.index(0), group].astype(F32)
-        for way in (1, -1):
-            handed(way, 3, group).wait_recv()
-            total += landed[0 if way == 1 else 1, 3, group].astype(F32)
+    def finish(pair):
+        for tile in (2 * pair, 2 * pair + 1):
+            make_terms(NEAREST_LAST.index(0), tile)
+            total = term[NEAREST_LAST.index(0), tile].astype(F32)
+            for way in (1, -1):
+                handed(way, 3, tile).wait_recv()
+                total += landed[0 if way == 1 else 1, 3, tile].astype(F32)
+            whole[tile % 2] = total
         for to in range(X):
-            mine = total[to * ROWS : (to + 1) * ROWS]
-            leaving[to, group] = jnp.concatenate([mine[:, :TILE], mine[:, TILE:]], axis=0).astype(BF16)
+            rows = slice(to * ROWS, (to + 1) * ROWS)
+            leaving[to, pair] = jnp.concatenate([whole[0, rows], whole[1, rows]], axis=0).astype(BF16)
         for step in range(1, X):
-            leave(group, step).start()
-        final[x, group] = leaving[x, group]
-
-    def write(group):
+            leave(pair, step).start()
+        final[x, pair] = leaving[x, pair]
+
+    def write(pair):
         for step in range(1, X):
-            leave(group, step).wait_recv()
+            leave(pair, step).wait_recv()
         for place in range(X):
-            total = final[place, group].astype(F32)
-            at = place * (D // X) + group * 2 * TILE
+            total = final[place, pair].astype(F32)
+            at = place * (D // X) + pair * 2 * TILE
             sums[0, :, at : at + TILE] = total[:ROWS]
             sums[0, :, at + TILE : at + 2 * TILE] = total[ROWS:]
 
-    def weights_of(half):
-        for tile in range(half * GROUPS, (half + 1) * GROUPS):
-            loads[3 + tile].wait()
-            for link in ("x+", "x-"):
-                need((link, 1, "W", tile))
-                if tile in FAR_TILES[link]:
-                    need((link, 1, "U", FAR_TILES[link].index(tile)))
-
-    def pass_context(j):
-        for link in ("x+", "x-"):
-            hand_context(link, 0, j).wait_recv()
-        for link in ("x+", "x-"):
-            hand_context(link, 1, j).start()
-            if j + 4 < Z:
-                hand_context(link, 0, j + 4).start()
-
-    for j in range(4):
-        for link in ("x+", "x-"):
-            hand_context(link, 0, j).start()
-    pass_context(0)
-    pass_context(1)
-    weights_of(0)
-    lagging = []
-    for i in range(Z):
-        for j in (2 * i + 2, 2 * i + 3):
-            if j < Z:
-                pass_context(j)
-        if 2 * i + 3 == Z - 1:
-            for tile in range(TILES // 2, TILES):
-                for link in ("x+", "x-"):
-                    weights((link, 1, "W", tile)).start()
-        for link in ("x+", "x-"):
-            hand_context(link, 1, i).wait_recv()
-        make_terms(i, 0)
-        now, later = ready_ones(i, 0)
-        for copy in now + lagging:
-            hand_on(*copy)
-        lagging = later
-    weights_of(1)
-    for i in range(Z):
-        make_terms(i, 1)
-        now, later = ready_ones(i, 1)
-        for copy in now + lagging:
-            hand_on(*copy)
-        lagging = later
-        if i == 3:
-            finish(1)
-            finish(0)
-        if i == 6:
-            write(1)
-            write(0)
-    for copy in lagging:
-        hand_on(*copy)
-    finish(3)
-    finish(2)
-
-    write(3)
-    write(2)
+    late = {}
+    late_tiles = {}
+    for link in ("x+", "x-"):
+        for i in range(Z):
+            late[link, 0, "P", i] = ((), BAND * WIDTH * 2)
+            late[link, 0, "Q", i] = (((link, 0, "P", i),), BAND * WIDTH)
+        for tile in range(TILES // 2, TILES):
+            key = (link, tile // 2 - 1, "W", tile)
+            late[key] = ((), WIDTH * TILE * 2)
+            late_tiles.setdefault(tile, []).append(key)
+        for i in range(EARLY_FAR, TILES // 2):
+            tile = FAR_TILES[link][i]
+            key = (link, tile // 2 - 1, "U", i)
+            late[key] = ((), WIDTH * TILE * 2)
+            late_tiles.setdefault(tile, []).append(key)
+    for way, link in ((1, "z+"), (-1, "z-")):
+        for tile in range(TILES):
+            rank = max(tile // 2 - 1, 0)
+            for step in range(4):
+                if step == 0 and starts_here(way, 1, tile):
+                    continue
+                away = way * (4 - step) if step else 4
+                wanted = [(l, 0, "Q", n) for l in ("x+", "x-") for n, a in enumerate(NEAREST_LAST) if abs(a) == abs(away)]
+                wanted += late_tiles.get(tile, [])
+                if not starts_here(way, step, tile):
+                    wanted.append((link, rank, "S", tile, step - 1))
+                late[link, rank, "S", tile, step] = (tuple(wanted), BAND * TILE * 2)
+    start, arrival = in_order(late, lambda key: 0.0)
+    here = set()
+
+    def need_late(key):
+        if key not in here:
+            here.add(key)
+            link, kind, i = key
+            if kind in "PQ":
+                hand_context(link, 0 if kind == "P" else 1, i).wait_recv()
+            else:
+                need((link, 1, kind, i))
+
+    events = [(t, 0, "copy", key) for key, t in start.items()]
+    for pair in range(PAIRS):
+        tiles = (2 * pair, 2 * pair + 1)
+        there = max(arrival[link, max(pair - 1, 0), "S", tile, 3] for link in ("z+", "z-") for tile in tiles)
+        events += [(there + 0.5, 1, "finish", pair), (there + 6.5, 2, "write", pair)]
+    events.sort(key=lambda event: event[:2])
+    for _, _, what, which in events:
+        if what == "finish":
+            finish(which)
+        elif what == "write":
+            write(which)
+        elif which[2] == "P":
+            hand_context(which[0], 0, which[3]).start()
+        elif which[2] == "Q":
+            need_late((which[0], "P", which[3]))
+            hand_context(which[0], 1, which[3]).start()
+        elif which[2] in "WU":
+            if which[2] == "U":
+                need((which[0], 1, "V", which[3]))
+            weights((which[0], 1, which[2], which[3])).start()
+        else:
+            link, _, _, tile, step = which
+            way = 1 if link == "z+" else -1
+            make_terms(NEAREST_LAST.index(way * (4 - step) if step else 4), tile)
+            hand_on(way, step, tile)
+
     for link in ("x+", "x-"):
         for i in range(TILES):
             weights((link, 1, "W", i)).wait_send()
@@ -615,13 +635,13 @@
             for hop in range(2):
                 hand_context(link, hop, i).wait_send()
     for way in (1, -1):
-        for group in range(GROUPS):
+        for tile in range(TILES):
             for step in range(4):
-                if step or group % 2 == (0 if way == 1 else 1):
-                    handed(way, step, group).wait_send()
-    for group in range(GROUPS):
+                if step or tile % 2 == (0 if way == 1 else 1):
+                    handed(way, step, tile).wait_send()
+    for pair in range(PAIRS):
         for step in range(1, X):
-            leave(group, step).wait_send()
+            leave(pair, step).wait_send()
 
 
 def layer(arriving, norm_gain, w_query, w_key, w_value, w_out):
@@ -655,10 +675,11 @@
             pltpu.VMEM((HD, LENGTH), BF16),
             pltpu.VMEM((Z, BAND, WIDTH), F32),
             pltpu.VMEM((X, Z, BAND, WIDTH), BF16),
-            pltpu.VMEM((Z, GROUPS, BAND, 2 * TILE), BF16),
-            pltpu.VMEM((2, 4, GROUPS, BAND, 2 * TILE), BF16),
-            pltpu.VMEM((X, GROUPS, 2 * ROWS, TILE), BF16),
-            pltpu.VMEM((X, GROUPS, 2 * ROWS, TILE), BF16),
+            pltpu.VMEM((Z, TILES, BAND, TILE), BF16),
+            pltpu.VMEM((2, 4, TILES, BAND, TILE), BF16),
+            pltpu.VMEM((2, BAND, TILE), F32),
+            pltpu.VMEM((X, PAIRS, 2 * ROWS, TILE), BF16),
+            pltpu.VMEM((X, PAIRS, 2 * ROWS, TILE), BF16),
             dma((3,)),
             dma((TILES,)),
             dma((2,)),
@@ -667,16 +688,16 @@
             dma((len(KEYS),)),
             dma((2, 2 * TILES)),
             dma((2, 2 * TILES)),
-            dma((1, X - 1)),
-            dma((1, X - 1)),
-            dma((1, Z - 1)),
-            dma((1, Z - 1)),
+            dma((3, X - 1)),
+            dma((3, X - 1)),
+            dma((3, Z - 1)),
+            dma((3, Z - 1)),
             dma((2, 2, Z)),
             dma((2, 2, Z)),
-            dma((2, 4, GROUPS)),
-            dma((2, 4, GROUPS)),
-            dma((X - 1, GROUPS)),
-            dma((X - 1, GROUPS)),
+            dma((2, 4, TILES)),
+            dma((2, 4, TILES)),
+            dma((X - 1, PAIRS)),
+            dma((X - 1, PAIRS)),
         ],
         compiler_params=pltpu.CompilerParams(
             collective_id=0, has_side_effects=True, vmem_limit_bytes=67043328

time: 163 us -> 159 us (0.975)
  Pallas kernels: 160 us -> 156 us
    pallas_call x1, Pallas kernels: 160 us -> 156 us  [layer(): pl.pallas_call(kernel, out_shape=(sums, entering), in_specs=[vmem, vmem,...]
where the time goes in v4:
time: 159 us
  Pallas kernels  156 us (98%)
  other arithmetic  2.44 us (2%)
    pallas_call x1, Pallas kernels, layer(): pl.pallas_call(kernel, out_shape=(sums, entering), in_specs=[vmem, vmem,...  156 us

profile of v4, /device:TPU:8, one launch (start us, length us, event | category | flops | bytes accessed | tf_op | source)
XLA Modules:
  0.0 158.8 jit_solution(2405746524450294583)
XLA Ops:
  0.6 155.7 %shard_map.77 = (f32[1,24,8192]{2,1,0:T(8,128)}, bf16[1,24,8192]{2,1,0:T(8,128)(2,1)}) custom-call(bf16[1,768,256]{2,1,0:T(8,128)(2,1)} %arriving.1, bf16[1,8192]{1,0:T(2,128)(2,1)} %gain.1, bf16[1,256,8192]{2,1,0:T(8,128)(2,1)} %w_query.1, bf16[1,32,8192]{2,1,0:T(8,128)(2,1)} %w_key.1, bf16[1,32,8192]{2,1,0:T(8,128)(2,1)} %w_value.1, ...), custom_call_target="tpu_custom_call" | custom-call | tf_op jit(solution)/shard_map/pallas_call | solution.py:653
  156.3 2.4 %add_convert_fusion = (bf16[1,24,8192]{2,1,0:T(8,128)(2,1)}, bf16[1,24,8192]{2,1,0:T(8,128)(2,1)}) fusion(f32[1,24,8192]{2,1,0:T(8,128)} %get-tuple-element.4, bf16[1,24,8192]{2,1,0:T(8,128)(2,1)} %get-tuple-element.5), kind=kLoop, calls=%fused_computation | loop fusion | flops 786432 | bytes 1966080 | tf_op jit(solution)/shard_map/convert_element_type | solution.py:706

commit v5 on v4

--- a/solution.py
+++ b/solution.py
@@ -117,11 +117,11 @@
 
 
 def kernel(
-    arriving, gain, w_query, w_key, w_value, w_out,
+    arriving_hbm, gain_hbm, w_query, w_key, w_value, w_out,
     sums, entering,
-    hidden, wq, wkv_raw, wkv, wo, stage, acc, squares, cos_q, sin_q, turn_kv, q_rot, own_kv, column_kv, all_kv, keys, values,
+    arriving, gain, hidden, wq, wkv_raw, wkv, wo, stage, acc, squares, cos_q, sin_q, turn_kv, q_rot, own_kv, column_kv, all_kv, keys, values,
     own_context, context, term, landed, whole, leaving, final,
-    w_sem, wo_sem, shift_send, shift_recv, gather_send, gather_recv, weight_send, weight_recv, x_send, x_recv, z_send, z_recv,
+    block_sem, w_sem, wo_sem, shift_send, shift_recv, gather_send, gather_recv, weight_send, weight_recv, x_send, x_recv, z_send, z_recv,
     context_send, context_recv, scatter_send, scatter_recv, final_send, final_recv,
 ):
     me = lax.axis_index("mp")
@@ -145,6 +145,10 @@
 
     for tile in range(TILES):
         loads.append(pltpu.make_async_copy(out_weights(x, tile), wo.at[tile, from_place(x)], wo_sem.at[tile]))
+    block_load = pltpu.make_async_copy(arriving_hbm, arriving, block_sem.at[0])
+    gain_load = pltpu.make_async_copy(gain_hbm, gain, block_sem.at[1])
+    block_load.start()
+    gain_load.start()
     for load in loads:
         load.start()
 
@@ -159,6 +163,7 @@
         )
     pl.semaphore_wait(barrier, (X - 1) + (Z - 1) + 2)
 
+    block_load.wait()
     parts = (GATHER_CUTS[0:3:2], GATHER_CUTS[2:5:2])
     shifts = []
     for s, (low, high) in enumerate(parts):
@@ -175,6 +180,7 @@
         )
         shifts[-1].start()
 
+    gain_load.wait()
     loads[0].wait()
     loads[1].wait()
     out_row = lax.broadcasted_iota(jnp.int32, (128, 64), 0)
@@ -291,7 +297,7 @@
                 tile = ready[8 * h : 8 * h + 8]
                 own_kv[h, t] = jnp.concatenate([tile[:, :128], tile[:, 128:]], axis=0).astype(BF16)
         these = pl.ds(blocks[n][0], len(blocks[n]))
-        for step in range(1, X):
+        for step in (2, 1, 3):
             to = lax.rem(x + step, X)
             copy = pltpu.make_async_remote_copy(
                 src_ref=own_kv.at[pl.ds(2 * to, 2), these],
@@ -310,7 +316,7 @@
         these = pl.ds(blocks[n][0], len(blocks[n]))
         for step in range(1, X):
             x_copies[n, step].wait_recv()
-        for step in range(1, Z):
+        for step in (4, 3, 5, 2, 6, 1, 7):
             to = lax.rem(z + step, Z)
             copy = pltpu.make_async_remote_copy(
                 src_ref=column_kv.at[:, to // 4, these],
@@ -555,7 +561,7 @@
         for step in range(1, X):
             leave(pair, step).wait_recv()
         for place in range(X):
-            total = final[place, pair].astype(F32)
+            total = final[place, pair]
             at = place * (D // X) + pair * 2 * TILE
             sums[0, :, at : at + TILE] = total[:ROWS]
             sums[0, :, at + TILE : at + 2 * TILE] = total[ROWS:]
@@ -644,18 +650,24 @@
             leave(pair, step).wait_send()
 
 
+def finish_kernel(summed, entering, attended, stream):
+    attended[...] = summed[...]
+    stream[...] = (entering[...].astype(F32) + summed[...].astype(F32)).astype(BF16)
+
+
 def layer(arriving, norm_gain, w_query, w_key, w_value, w_out):
     any_space = pl.BlockSpec(memory_space=pl.ANY)
     vmem = pl.BlockSpec(memory_space=pltpu.VMEM)
-    sums = jax.ShapeDtypeStruct((1, ROWS, D), F32)
-    entering = jax.ShapeDtypeStruct((1, ROWS, D), BF16)
+    out = jax.ShapeDtypeStruct((1, ROWS, D), BF16)
     dma = pltpu.SemaphoreType.DMA
     summed, residual = pl.pallas_call(
         kernel,
-        out_shape=(sums, entering),
-        in_specs=[vmem, vmem, any_space, any_space, any_space, any_space],
+        out_shape=(out, out),
+        in_specs=[any_space, any_space, any_space, any_space, any_space, any_space],
         out_specs=(vmem, vmem),
         scratch_shapes=[
+            pltpu.VMEM((1, LENGTH, WIDTH), BF16),
+            pltpu.VMEM((1, D), BF16),
             pltpu.VMEM((N, LENGTH, WIDTH), BF16),
             pltpu.VMEM((WIDTH, D), BF16),
             pltpu.VMEM((2, 32, D), BF16),
@@ -680,6 +692,7 @@
             pltpu.VMEM((2, BAND, TILE), F32),
             pltpu.VMEM((X, PAIRS, 2 * ROWS, TILE), BF16),
             pltpu.VMEM((X, PAIRS, 2 * ROWS, TILE), BF16),
+            dma((2,)),
             dma((3,)),
             dma((TILES,)),
             dma((2,)),
@@ -703,7 +716,7 @@
             collective_id=0, has_side_effects=True, vmem_limit_bytes=67043328
         ),
     )(arriving, norm_gain, w_query, w_key, w_value, w_out)
-    return summed.astype(BF16), (residual.astype(F32) + summed).astype(BF16)
+    return pl.pallas_call(finish_kernel, out_shape=(out, out), in_specs=[vmem, vmem], out_specs=(vmem, vmem))(summed, residual)
 
 
 def solution(mesh):

time: 159 us -> 157 us (0.987)
  other arithmetic: 2.44 us -> 0 us
    convert_element_type x1 -> x0, other arithmetic: 2.44 us -> none  [layer(): return (summed.astype(BF16), (residual.astype(F32) + summed).astype(BF16))]
    pallas_call x1 -> x2, Pallas kernels: 156 us -> 156 us  [the longest x1 154 us: layer(): pl.pallas_call(kernel, out_shape=(out, out), in_specs=[any_space, any_spa...]
where the time goes in v5:
time: 157 us
  Pallas kernels  156 us (99%)
    pallas_call x1, Pallas kernels, layer(): pl.pallas_call(kernel, out_shape=(out, out), in_specs=[any_space, any_spa...  154 us

profile of v5, /device:TPU:8, one launch (start us, length us, event | category | flops | bytes accessed | tf_op | source)
XLA Modules:
  0.0 156.9 jit_solution(10958670824701962965)
XLA Ops:
  0.6 154.2 %shard_map.77 = (bf16[1,24,8192]{2,1,0:T(8,128)(2,1)}, bf16[1,24,8192]{2,1,0:T(8,128)(2,1)}) custom-call(bf16[1,768,256]{2,1,0:T(8,128)(2,1)} %arriving_hbm.1, bf16[1,8192]{1,0:T(2,128)(2,1)} %gain_hbm.1, bf16[1,256,8192]{2,1,0:T(8,128)(2,1)} %w_query.1, bf16[1,32,8192]{2,1,0:T(8,128)(2,1)} %w_key.1, bf16[1,32,8192]{2,1,0:T(8,128)(2,1)} %w_value.1, ...), custom_call_target="tpu_custom_call" | custom-call | tf_op jit(solution)/shard_map/pallas_call | solution.py:663
  154.9 2.0 %shard_map.78 = (bf16[1,24,8192]{2,1,0:T(8,128)(2,1)}, bf16[1,24,8192]{2,1,0:T(8,128)(2,1)}) custom-call(bf16[1,24,8192]{2,1,0:T(8,128)(2,1)} %get-tuple-element.4.summed, bf16[1,24,8192]{2,1,0:T(8,128)(2,1)} %get-tuple-element.5.entering), custom_call_target="tpu_custom_call" | custom-call | tf_op jit(solution)/shard_map/pallas_call | solution.py:719

commit v6 on v5

--- a/solution.py
+++ b/solution.py
@@ -153,15 +153,15 @@
         load.start()
 
     barrier = pltpu.get_barrier_semaphore()
-    for step in range(1, X):
+    for step in (1, X - 1):
         pl.semaphore_signal(barrier, inc=1, device_id={"mp": near(step, 0)}, device_id_type=MESH)
-    for step in range(1, Z):
+    for step in (1, Z - 1):
         pl.semaphore_signal(barrier, inc=1, device_id={"mp": near(0, step)}, device_id_type=MESH)
     for step in (1, SECTIONS - 1):
         pl.semaphore_signal(
             barrier, inc=1, device_id={"section": lax.rem(section + step, SECTIONS)}, device_id_type=MESH
         )
-    pl.semaphore_wait(barrier, (X - 1) + (Z - 1) + 2)
+    pl.semaphore_wait(barrier, 6)
 
     block_load.wait()
     parts = (GATHER_CUTS[0:3:2], GATHER_CUTS[2:5:2])

time: 157 us -> 157 us (level)
  no operation moved by 1% of the time
where the time goes in v6:
time: 157 us
  Pallas kernels  156 us (99%)
    pallas_call x1, Pallas kernels, layer(): pl.pallas_call(kernel, out_shape=(out, out), in_specs=[any_space, any_spa...  154 us

profile of v6, /device:TPU:8, one launch (start us, length us, event | category | flops | bytes accessed | tf_op | source)
XLA Modules:
  0.0 156.8 jit_solution(8252461004818598485)
XLA Ops:
  0.6 154.2 %shard_map.77 = (bf16[1,24,8192]{2,1,0:T(8,128)(2,1)}, bf16[1,24,8192]{2,1,0:T(8,128)(2,1)}) custom-call(bf16[1,768,256]{2,1,0:T(8,128)(2,1)} %arriving_hbm.1, bf16[1,8192]{1,0:T(2,128)(2,1)} %gain_hbm.1, bf16[1,256,8192]{2,1,0:T(8,128)(2,1)} %w_query.1, bf16[1,32,8192]{2,1,0:T(8,128)(2,1)} %w_key.1, bf16[1,32,8192]{2,1,0:T(8,128)(2,1)} %w_value.1, ...), custom_call_target="tpu_custom_call" | custom-call | tf_op jit(solution)/shard_map/pallas_call | solution.py:663
  154.8 2.0 %shard_map.78 = (bf16[1,24,8192]{2,1,0:T(8,128)(2,1)}, bf16[1,24,8192]{2,1,0:T(8,128)(2,1)}) custom-call(bf16[1,24,8192]{2,1,0:T(8,128)(2,1)} %get-tuple-element.4.summed, bf16[1,24,8192]{2,1,0:T(8,128)(2,1)} %get-tuple-element.5.entering), custom_call_target="tpu_custom_call" | custom-call | tf_op jit(solution)/shard_map/pallas_call | solution.py:719
